TPU v7x, 8 devices: a whole 2x2x1 slice. The times are simulated.
8 devices in a mesh: rep: 2 (over y, z), dp: 4 (over x, core).
Axes of the slice: x: 2, y: 2, z: 1, core: 2. Of those that a mesh axis runs over, the one named last changes fastest.
Arguments:
- x: bfloat16 [8, 2048, 768], P(('rep', 'dp')), parts along dimension 0
- dy: bfloat16 [8, 2048, 768], P(('rep', 'dp')), parts along dimension 0
- w_gate: bfloat16 [2, 768, 6144], replicated
- w_up: bfloat16 [2, 768, 6144], replicated
- w_down: bfloat16 [2, 6144, 768], replicated
- m_w_gate: float32 [2, 768, 6144], replicated
- m_w_up: float32 [2, 768, 6144], replicated
- m_w_down: float32 [2, 6144, 768], replicated
- v_w_gate: float32 [2, 768, 6144], replicated
- v_w_up: float32 [2, 768, 6144], replicated
- v_w_down: float32 [2, 6144, 768], replicated
Outputs:
- output 1: bfloat16 [4, 768, 6144], P('rep'), parts along dimension 0
- output 2: bfloat16 [4, 768, 6144], P('rep'), parts along dimension 0
- output 3: bfloat16 [4, 6144, 768], P('rep'), parts along dimension 0
- output 4: float32 [4, 768, 6144], P('rep'), parts along dimension 0
- output 5: float32 [4, 768, 6144], P('rep'), parts along dimension 0
- output 6: float32 [4, 6144, 768], P('rep'), parts along dimension 0
- output 7: float32 [4, 768, 6144], P('rep'), parts along dimension 0
- output 8: float32 [4, 768, 6144], P('rep'), parts along dimension 0
- output 9: float32 [4, 6144, 768], P('rep'), parts along dimension 0
There are 2 independent parts. A program takes and returns all parts, laid end to end along the dimension named above; an argument that names none is the same for every part.
All inputs are finite; a program needn't handle non-finite values.
Results may differ from a plain program's by a relative error of at most 0.0246.
Values are sent between devices in bfloat16 or wider.
A program may use at most 3 GiB of HBM per device.

v0:
```python
import jax
import jax.numpy as jnp
from jax import lax
from jax.sharding import PartitionSpec as P

NAMES = ("w_gate", "w_up", "w_down")


def matmul(a, w):
    return jnp.dot(a, w, preferred_element_type=jnp.float32).astype(jnp.bfloat16)


def normed(h):
    wide = h.astype(jnp.float32)
    scale = lax.rsqrt(jnp.mean(wide**2, -1, keepdims=True) + 1e-6)
    return (wide * scale).astype(jnp.bfloat16)


def layer(h, w):
    a = normed(h)
    gate = jnp.dot(a, w["w_gate"], preferred_element_type=jnp.float32)
    up = jnp.dot(a, w["w_up"], preferred_element_type=jnp.float32)
    return h + matmul((jax.nn.silu(gate) * up).astype(jnp.bfloat16), w["w_down"])


def adamw(w, m, v, g):
    m = 0.9 * m + 0.1 * g
    v = 0.95 * v + 0.05 * g * g
    step = m * lax.rsqrt(v + 1e-8) + 0.1 * w
    return (w - 0.02 * step).astype(jnp.bfloat16), m, v


def solution(mesh):
    def step(x, dy, *arrays):
        weights, m, v = (arrays[i : i + 3] for i in (0, 3, 6))
        layers = weights[0].shape[0]
        h, kept = x[0], []
        for number in range(layers):
            kept.append(h)
            h = layer(h, {name: w[number] for name, w in zip(NAMES, weights, strict=True)})
        by_h, summed = dy[0], [None] * layers
        for number in reversed(range(layers)):
            _, back = jax.vjp(lambda w, h: layer(h, w), {name: w[number] for name, w in zip(NAMES, weights, strict=True)}, kept[number])
            by_w, by_h = back(by_h)
            summed[number] = [lax.psum(by_w[name], "dp") for name in NAMES]
        gradients = [jnp.stack([summed[number][i] for number in range(layers)]).astype(jnp.float32) for i in range(3)]
        new = [adamw(w.astype(jnp.float32), m, v, g) for w, m, v, g in zip(weights, m, v, gradients, strict=True)]
        return tuple(one[which] for which in range(3) for one in new)

    return jax.shard_map(
        step,
        mesh=mesh,
        in_specs=(P(("rep", "dp"), None, None),) * 2 + (P(None, None, None),) * 9,
        out_specs=(P("rep", None, None),) * 9,
        check_vma=False,
    )
```

profile of v0, /device:TPU:0, one launch (start us, length us, event | category | flops | bytes accessed | tf_op | source)
XLA Modules:
  0.0 1676.5 jit_solution(13145643292358819360)
XLA Ops:
  7.2 0.0 all-reduce.3.cloned.1.call-start
  7.2 3.2 copy.20
  10.4 0.0 copy-start
  10.4 0.7 fusion.69
  11.1 0.0 copy-start.11
  11.1 5.1 copy.21
  16.2 0.0 copy-start.4
  16.2 26.6 %convolution_convert_fusion.1 = bf16[2048,6144]{1,0:T(8,128)(2,1)} fusion(bf16[2,6144,768]{2,1,0:T(8,128)(2,1)} %param.15, bf16[1,2048,768]{2,1,0:T(8,128)(2,1)} %param.12), kind=kOutput, calls=%fused_computation.52 | convolution fusion | flops 19339935744 | bytes 37748736 | tf_op jit(solution)/shard_map/transpose(jvp())/dot_general | solution.py:10
  42.9 0.0 copy-done
  42.9 0.0 copy-done.4
  42.9 28.9 %fusion.49 = f32[2048,6144]{1,0:T(8,128)} fusion(bf16[2,768,6144]{2,1,0:T(8,128)(2,1)} %param.13, bf16[1,2048,768]{2,1,0:T(8,128)(2,1)S(1)} %copy-done.4, f32[2048]{0:T(1024)S(1)} %add_rsqrt_fusion), kind=kOutput, calls=%fused_computation.79 | convolution fusion | flops 19332071424 | bytes 62922752 | tf_op jit(solution)/shard_map/dot_general | solution.py:21
  71.8 0.0 copy-done.11
  71.8 0.0 copy-start.1
  71.8 49.3 %multiply_convert_fusion.1 = (bf16[2048,6144]{1,0:T(8,128)(2,1)}, f32[2048,6144]{1,0:T(8,128)}) fusion(f32[2048,6144]{1,0:T(8,128)} %fusion.49, bf16[2,768,6144]{2,1,0:T(8,128)(2,1)} %param.14, bf16[1,2048,768]{2,1,0:T(8,128)(2,1)} %param.11, f32[2048]{0:T(1024)S(1)} %add_rsqrt_fusion), kind=kOutput, calls=%fused_computation.20 | convolution fusion | flops 19407568896 | bytes 138420224 | tf_op jit(solution)/shard_map/dot_general | solution.py:22
  121.0 0.0 copy-done.1
  121.0 26.9 %fusion.73 = (f32[2048]{0:T(1024)S(1)}, bf16[2048,768]{0,1:T(8,128)(2,1)}) fusion(bf16[2048,6144]{1,0:T(8,128)(2,1)} %get-tuple-element.24, bf16[2,6144,768]{2,1,0:T(8,128)(2,1)} %param.15, bf16[1,2048,768]{1,2,0:T(8,128)(2,1)S(1)} %copy-done.1), kind=kOutput, calls=%fused_computation.103 | convolution fusion | flops 19335215104 | bytes 40902656 | tf_op jit(solution)/shard_map/dot_general | solution.py:10
  148.0 0.0 copy-start.9
  148.0 0.0 copy-start.6
  148.0 29.9 %fusion.36 = f32[2048,6144]{1,0:T(8,128)} fusion(bf16[2,768,6144]{2,1,0:T(8,128)(2,1)} %param.14, bf16[2048,768]{0,1:T(8,128)(2,1)} %get-tuple-element.27, f32[2048]{0:T(1024)S(1)} %fusion.102), kind=kOutput, calls=%fused_computation.66 | convolution fusion | flops 19332071424 | bytes 62922752 | tf_op jit(solution)/shard_map/jvp()/dot_general | solution.py:22
  177.9 0.0 copy-done.9
  177.9 0.0 copy-done.6
  177.9 64.0 %fusion.2 = (bf16[2048,6144]{1,0:T(8,128)(2,1)}, f32[2048,6144]{1,0:T(8,128)}) fusion(f32[2048,6144]{1,0:T(8,128)} %fusion.36, bf16[2048,6144]{1,0:T(8,128)(2,1)} %convolution_convert_fusion.1, bf16[2,768,6144]{2,1,0:T(8,128)(2,1)} %param.13, bf16[2048,768]{0,1:T(8,128)(2,1)S(1)} %copy-done.6, f32[2048]{0:T(1024)S(1)} %fusion.102), kind=kOutput, calls=%fused_computation.11 | convolution fusion | flops 19483066368 | bytes 163586048 | tf_op jit(solution)/shard_map/jvp()/dot_general | solution.py:21
  241.9 33.1 %fusion.76 = bf16[2048,768]{0,1:T(8,128)(2,1)} fusion(bf16[2,768,6144]{2,1,0:T(8,128)(2,1)} %param.14, bf16[2048,6144]{1,0:T(8,128)(2,1)} %convolution_convert_fusion.1, f32[2048,6144]{1,0:T(8,128)} %get-tuple-element.29), kind=kOutput, calls=%fused_computation.107 | convolution fusion | flops 19404423168 | bytes 88080384 | tf_op jit(solution)/shard_map/transpose(jvp())/dot_general | solution.py:22
  275.0 0.0 copy-start.5
  275.0 33.0 %fusion.56 = bf16[1,768,6144]{2,1,0:T(8,128)(2,1)} fusion(bf16[2048,6144]{1,0:T(8,128)(2,1)} %convolution_convert_fusion.1, bf16[2048,768]{0,1:T(8,128)(2,1)} %get-tuple-element.27, f32[2048]{0:T(1024)S(1)} %fusion.102, f32[2048,6144]{1,0:T(8,128)} %get-tuple-element.29), kind=kOutput, calls=%fused_computation.86 | convolution fusion | flops 19412287488 | bytes 88088576 | tf_op jit(solution)/shard_map/transpose(jvp())/dot_general | solution.py:22
  308.0 0.0 copy-done.5
  308.0 42.2 %fusion.61 = bf16[1,6144,768]{2,1,0:T(8,128)(2,1)} fusion(f32[2048,6144]{1,0:T(8,128)} %fusion.36, bf16[1,2048,768]{2,1,0:T(8,128)(2,1)S(1)} %copy-done.5, f32[2048,6144]{1,0:T(8,128)} %get-tuple-element.29), kind=kOutput, calls=%fused_computation.89 | convolution fusion | flops 19407568896 | bytes 113246208 | tf_op jit(solution)/shard_map/transpose(jvp())/dot_general | solution.py:10
  350.2 0.0 copy-start.7
  350.2 26.1 %fusion.57 = bf16[1,768,6144]{2,1,0:T(8,128)(2,1)} fusion(bf16[2048,6144]{1,0:T(8,128)(2,1)} %get-tuple-element.28, bf16[2048,768]{0,1:T(8,128)(2,1)} %get-tuple-element.27, f32[2048]{0:T(1024)S(1)} %fusion.102), kind=kOutput, calls=%fused_computation.87 | convolution fusion | flops 19332071424 | bytes 37756928 | tf_op jit(solution)/shard_map/transpose(jvp())/dot_general | solution.py:21
  376.3 0.0 copy-done.7
  376.3 0.0 copy-start.10
  376.3 0.0 copy-start.3
  376.3 27.7 %fusion.75 = (f32[2048]{0:T(1024)S(1)}, bf16[2048,768]{0,1:T(8,128)(2,1)}) fusion(bf16[2048,768]{0,1:T(8,128)(2,1)S(1)} %copy-done.7, bf16[2048,768]{0,1:T(8,128)(2,1)} %fusion.76, bf16[2048,6144]{1,0:T(8,128)(2,1)} %get-tuple-element.28, bf16[2,768,6144]{2,1,0:T(8,128)(2,1)} %param.13), kind=kOutput, calls=%fused_computation.105 | convolution fusion | flops 19335215104 | bytes 44048384 | tf_op jit(solution)/shard_map/transpose(jvp())/dot_general | solution.py:21
  404.0 0.0 copy-done.10
  404.0 0.0 copy-done.3
  404.0 5.8 fusion.86
  409.8 0.0 copy-start.8
  409.8 27.5 %convolution_convert_fusion = bf16[2048,6144]{1,0:T(8,128)(2,1)} fusion(bf16[2048,768]{0,1:T(8,128)(2,1)} %fusion.86, bf16[2,6144,768]{2,1,0:T(8,128)(2,1)} %param.15), kind=kOutput, calls=%fused_computation.51 | convolution fusion | flops 19339935744 | bytes 37748736 | tf_op jit(solution)/shard_map/transpose(jvp())/dot_general | solution.py:10
  437.4 0.0 copy-done.8
  437.4 0.0 copy-start.2
  437.4 0.0 copy-start.12
  437.4 26.9 %fusion.54 = bf16[1,6144,768]{2,1,0:T(8,128)(2,1)} fusion(bf16[2048,6144]{1,0:T(8,128)(2,1)} %get-tuple-element.24, bf16[2048,768]{0,1:T(8,128)(2,1)S(1)} %copy-done.8), kind=kOutput, calls=%fused_computation.84 | convolution fusion | flops 19332071424 | bytes 37748736 | tf_op jit(solution)/shard_map/transpose(jvp())/dot_general | solution.py:10
  464.3 0.0 copy-done.2
  464.3 0.0 copy-done.12
  464.3 32.3 %fusion.55 = bf16[1,768,6144]{2,1,0:T(8,128)(2,1)} fusion(bf16[2048,6144]{1,0:T(8,128)(2,1)} %convolution_convert_fusion, f32[2048,6144]{1,0:T(8,128)} %fusion.49, bf16[1,2048,768]{1,2,0:T(8,128)(2,1)S(1)} %copy-done.2, f32[2048]{0:T(1024)S(1)} %copy-done.12), kind=kOutput, calls=%fused_computation.85 | convolution fusion | flops 19412287488 | bytes 88088576 | tf_op jit(solution)/shard_map/transpose(jvp())/dot_general | solution.py:22
  496.6 47.0 %fusion.58 = bf16[1,768,6144]{2,1,0:T(8,128)(2,1)} fusion(f32[2048,6144]{1,0:T(8,128)} %fusion.49, f32[2048,6144]{1,0:T(8,128)} %get-tuple-element.25, bf16[2048,6144]{1,0:T(8,128)(2,1)} %convolution_convert_fusion, bf16[1,2048,768]{1,2,0:T(8,128)(2,1)S(1)} %copy-done.2, f32[2048]{0:T(1024)S(1)} %copy-done.12), kind=kOutput, calls=%fused_computation.88 | convolution fusion | flops 19475202048 | bytes 138420224 | tf_op jit(solution)/shard_map/transpose(jvp())/dot_general | solution.py:21
  543.6 0.0 all-reduce.3.cloned.1.call-update
  543.6 925.9 %all-reduce.3.cloned.1.call-done = (bf16[1,768,6144]{2,1,0:T(8,128)(2,1)}, bf16[1,768,6144]{2,1,0:T(8,128)(2,1)}, bf16[1,768,6144]{2,1,0:T(8,128)(2,1)}, bf16[1,...) async-done(((bf16[1,768,6144]{2,1,0:T(8,128)(2,1)}, bf16[1,768,6144]{2,1,0:T(8,128)(2,1)}, bf16[1,768,6144]{2,1,0:T(8,128)(2,1)}, ...) | async-done | bytes 56623120 | tf_op jit(solution)/shard_map/psum | solution.py:45
  1469.5 69.2 %fusion.21 = (bf16[2,6144,768]{2,1,0:T(8,128)(2,1)}, f32[2,6144,768]{2,1,0:T(8,128)}, f32[2,6144,768]{2,1,0:T(8,128)}) fusion(bf16[2,6144,768]{2,1,0:T(8,128)(2,1)} %param.15, bf16[1,6144,768]{2,1,0:T(8,128)(2,1)} %get-tuple-element.13, bf16[1,6144,768]{2,1,0:T(8,128)(2,1)} %get-tuple-element.14, f32[2,6144,768]{2,1,0:T(8,128)} %param.21, ...), kind=kLoop, calls=%fused_computation.42 | loop fusion | flops 179306496 | bytes 207618048 | tf_op jit(solution)/shard_map/convert_element_type | solution.py:30
  1538.8 130.3 %fusion.13 = (bf16[2,768,6144]{2,1,0:T(8,128)(2,1)}, f32[2,768,6144]{2,1,0:T(8,128)}, f32[2,768,6144]{2,1,0:T(8,128)}, bf16[2,768,6144]{2,1,0:T(8,128)(2,1)}, f3...) fusion(bf16[2,768,6144]{2,1,0:T(8,128)(2,1)} %param.13, bf16[1,768,6144]{2,1,0:T(8,128)(2,1)} %get-tuple-element.9, ...), kind=kLoop, calls=%fused_computation.34 | loop fusion | flops 358612992 | bytes 415236096 | tf_op jit(solution)/shard_map/convert_element_type | solution.py:30
  (3 shorter events, 0.0 us)
Async XLA Ops:
  7.2 1462.4 %all-reduce.3.cloned.1.call-start = ((), (), s32[]{:S(2)}) async-start(), calls=%async_computation | async-start | bytes 113246208 | tf_op jit(solution)/shard_map/psum | solution.py:45
  10.4 32.4 %copy-start = (bf16[1,2048,768]{1,2,0:T(8,128)(2,1)}, bf16[1,2048,768]{1,2,0:T(8,128)(2,1)S(1)}, u32[]{:S(2)}) copy-start(bf16[1,2048,768]{1,2,0:T(8,128)(2,1)S(1)} %copy.20) | copy-start | bytes 9437188
  11.1 60.7 %copy-start.11 = (f32[2048]{0:T(1024)}, f32[2048]{0:T(1024)S(1)}, u32[]{:S(2)}) copy-start(f32[2048]{0:T(1024)S(1)} %add_rsqrt_fusion) | copy-start | bytes 24580
  16.2 26.6 %copy-start.4 = (bf16[1,2048,768]{2,1,0:T(8,128)(2,1)S(1)}, bf16[1,2048,768]{2,1,0:T(8,128)(2,1)}, u32[]{:S(2)}) copy-start(bf16[1,2048,768]{2,1,0:T(8,128)(2,1)} %param.11) | copy-start | bytes 9437188
  71.8 49.3 %copy-start.1 = (bf16[1,2048,768]{1,2,0:T(8,128)(2,1)S(1)}, bf16[1,2048,768]{1,2,0:T(8,128)(2,1)}, u32[]{:S(2)}) copy-start(bf16[1,2048,768]{1,2,0:T(8,128)(2,1)} %copy-done) | copy-start | bytes 9437188
  148.0 29.9 %copy-start.9 = (f32[2048]{0:T(1024)}, f32[2048]{0:T(1024)S(1)}, u32[]{:S(2)}) copy-start(f32[2048]{0:T(1024)S(1)} %get-tuple-element.26) | copy-start | bytes 24580
  148.0 29.9 %copy-start.6 = (bf16[2048,768]{0,1:T(8,128)(2,1)S(1)}, bf16[2048,768]{0,1:T(8,128)(2,1)}, u32[]{:S(2)}) copy-start(bf16[2048,768]{0,1:T(8,128)(2,1)} %get-tuple-element.27) | copy-start | bytes 9437188
  275.0 33.0 %copy-start.5 = (bf16[1,2048,768]{2,1,0:T(8,128)(2,1)S(1)}, bf16[1,2048,768]{2,1,0:T(8,128)(2,1)}, u32[]{:S(2)}) copy-start(bf16[1,2048,768]{2,1,0:T(8,128)(2,1)} %param.12) | copy-start | bytes 9437188
  350.2 26.1 %copy-start.7 = (bf16[2048,768]{0,1:T(8,128)(2,1)S(1)}, bf16[2048,768]{0,1:T(8,128)(2,1)}, u32[]{:S(2)}) copy-start(bf16[2048,768]{0,1:T(8,128)(2,1)} %get-tuple-element.27) | copy-start | bytes 9437188
  376.3 27.7 %copy-start.10 = (f32[2048]{0:T(1024)S(1)}, f32[2048]{0:T(1024)}, u32[]{:S(2)}) copy-start(f32[2048]{0:T(1024)} %copy-done.9) | copy-start | bytes 24580
  376.3 27.7 %copy-start.3 = (bf16[1,2048,768]{1,2,0:T(8,128)(2,1)S(1)}, bf16[1,2048,768]{1,2,0:T(8,128)(2,1)}, u32[]{:S(2)}) copy-start(bf16[1,2048,768]{1,2,0:T(8,128)(2,1)} %copy.21) | copy-start | bytes 9437188
  409.8 27.5 %copy-start.8 = (bf16[2048,768]{0,1:T(8,128)(2,1)S(1)}, bf16[2048,768]{0,1:T(8,128)(2,1)}, u32[]{:S(2)}) copy-start(bf16[2048,768]{0,1:T(8,128)(2,1)} %fusion.86) | copy-start | bytes 9437188
  437.4 26.9 %copy-start.2 = (bf16[1,2048,768]{1,2,0:T(8,128)(2,1)S(1)}, bf16[1,2048,768]{1,2,0:T(8,128)(2,1)}, u32[]{:S(2)}) copy-start(bf16[1,2048,768]{1,2,0:T(8,128)(2,1)} %copy-done) | copy-start | bytes 9437188
  437.4 26.9 %copy-start.12 = (f32[2048]{0:T(1024)S(1)}, f32[2048]{0:T(1024)}, u32[]{:S(2)}) copy-start(f32[2048]{0:T(1024)} %copy-done.11) | copy-start | bytes 24580
Sparse Core Ops, SparseCore 0:
  543.8 925.7 all-reduce.2
where the time goes:
time: 1680 us
  waiting for transfers between devices  926 us (55%)
  matrix products  521 us (31%)
  other arithmetic  206 us (12%)
    psum x1, waiting for transfers between devices, step(): summed[number] = [lax.psum(by_w[name], 'dp') for name in NAMES]  926 us
    convert_element_type x2, other arithmetic, adamw(): return ((w - 0.02 * step).astype(jnp.bfloat16), m, v)  200 us
    dot_general x5, matrix products, layer(): gate = jnp.dot(a, w['w_gate'], preferred_element_type=jnp.float32)  194 us
    dot_general x5, matrix products, layer(): up = jnp.dot(a, w['w_up'], preferred_element_type=jnp.float32)  177 us
    dot_general x5, matrix products, matmul(): jnp.dot(a, w, preferred_element_type=jnp.float32).astype(jnp.bfloat16)  150 us
  transfers between devices with their start and end apart: 1, of which 1 were waited for; matrix products, arithmetic and copies ran while one was open for 0% of the time, Pallas kernels for 0%

commit v1 on v0

v1 whole, which is shorter than its diff:
```python
import functools

import jax
import jax.numpy as jnp
from jax import lax
from jax.experimental import pallas as pl
from jax.experimental.pallas import tpu as pltpu
from jax.sharding import PartitionSpec as P


BF, F32 = jnp.bfloat16, jnp.float32
AXES = ("rep", "dp")
MESH = pl.DeviceIdType.MESH
CHUNK = 512
ROWS = 512
ADAM_COLS = 256
VMEM = 60 << 20
NX = 5


def sigmoid(x):
    return pl.reciprocal(1.0 + jnp.exp(-x), approx=False)

def nn(a, b):
    return jnp.dot(a, b, preferred_element_type=F32)

def nt(a, b):
    return lax.dot_general(a, b, (((1,), (1,)), ((), ())), preferred_element_type=F32)

def tn(a, b):
    return lax.dot_general(a, b, (((0,), (0,)), ((), ())), preferred_element_type=F32)

def scale_of(wide):
    return lax.rsqrt(jnp.mean(wide * wide, -1, keepdims=True) + 1e-6)

def normed(h):
    wide = h.astype(F32)
    return (wide * scale_of(wide)).astype(BF)

def forward_kernel(rows_, h_ref, wg_ref, wu_ref, wd_ref, out_ref, a_ref, next_ref, gate_ref, up_ref, acc_ref):
    step = pl.program_id(0)

    @pl.when(step == 0)
    def _():
        a_ref[...] = normed(h_ref[...])
        acc_ref[...] = jnp.zeros_like(acc_ref)

    for r in range(h_ref.shape[0] // rows_):
        rows = pl.ds(r * rows_, rows_)
        a = a_ref[rows]
        gate = nn(a, wg_ref[...])
        up = nn(a, wu_ref[...])
        gate_ref[rows] = gate
        up_ref[rows] = up
        p = (gate * sigmoid(gate) * up).astype(BF)
        acc_ref[rows] += nn(p, wd_ref[...])

    @pl.when(step == pl.num_programs(0) - 1)
    def _():
        h = h_ref[...] + acc_ref[...].astype(BF)
        out_ref[...] = h
        next_ref[...] = normed(h)

def forward(h, wg, wu, wd, layer, chunk=512, rows=512):
    t, d = h.shape
    ff = wg.shape[2]
    full = pl.BlockSpec((t, d), lambda j: (0, 0))
    wide = pl.BlockSpec((None, d, chunk), lambda j: (layer, 0, j))
    cols = pl.BlockSpec((t, chunk), lambda j: (0, j))
    return pl.pallas_call(
        functools.partial(forward_kernel, rows),
        grid=(ff // chunk,),
        in_specs=[full, wide, wide, pl.BlockSpec((None, chunk, d), lambda j: (layer, j, 0))],
        out_specs=[full] * 3 + [cols] * 2,
        out_shape=[jax.ShapeDtypeStruct((t, d), BF)] * 3 + [jax.ShapeDtypeStruct((t, ff), F32)] * 2,
        scratch_shapes=[pltpu.VMEM((t, d), F32)],
        compiler_params=pltpu.CompilerParams(vmem_limit_bytes=VMEM),
        cost_estimate=pl.CostEstimate(flops=6 * t * d * ff, bytes_accessed=8 * t * ff, transcendentals=0),
        name="forward",
    )(h, wg, wu, wd)

def middle(gate, up, dp, rows, p_s, dg_s, du_s):
    dp = dp.astype(BF).astype(F32)
    s = sigmoid(gate)
    silu = gate * s
    p_s[rows] = (silu * up).astype(BF)
    du_s[rows] = (dp * silu).astype(BF)
    dg_s[rows] = (dp * up * (s + silu * (1.0 - s))).astype(BF)

def both_kernel(nx, a1, h1, dy, a0, wg, wu, wd, gate0, up0, *refs):
    n = 2 * (wd.shape[1] // 2 // CHUNK)
    refs = list(refs)
    take = lambda k: [refs.pop(0) for _ in range(k)]
    sums, came = take(n), take(nx)
    (landed,) = take(1)
    a_v, dy_v, b_v, da_v, p_s, dg_s, du_s, wg_v, wu_v, wd_v, gate_v, up_v, add_v, grad_v = take(14)
    in_sem, w_sem, g_sem, add_sem, out_sem, d_send, d_recv, x_send, x_recv = take(9)
    per = n // 2
    half_steps = 2 * per
    steps = 2 * half_steps
    j = pl.program_id(0)
    rep, dp = lax.axis_index("rep"), lax.axis_index("dp")
    core = lax.rem(dp, 2)
    beside = (rep, dp + 1 - 2 * core)
    across = (rep, lax.rem(dp + 2, 4))
    t = a_v.shape[0]

    def what(j):
        layer = j // half_steps
        k = lax.rem(j, half_steps)
        own = ((k >= 2) & (lax.rem(k, 2) == 0)) | (k == half_steps - 1)
        number = jnp.where(own, jnp.where(k == half_steps - 1, per - 1, k // 2 - 1), (k + 1) // 2)
        return layer, own, number, layer * per + number

    def columns(j):
        _, own, number, _ = what(j)
        side = jnp.where(own, core, 1 - core)
        return pl.ds(pl.multiple_of((side * per + number) * CHUNK, CHUNK), CHUNK)

    def loads(j, top):
        s = lax.rem(j, 2)
        cols = columns(j)
        if top:
            return [
                pltpu.make_async_copy(wg.at[1, :, cols], wg_v.at[s], w_sem.at[s, 0]),
                pltpu.make_async_copy(wu.at[1, :, cols], wu_v.at[s], w_sem.at[s, 1]),
                pltpu.make_async_copy(wd.at[1, cols], wd_v.at[s], w_sem.at[s, 2]),
            ]
        return [
            pltpu.make_async_copy(gate0.at[:, cols], gate_v.at[s], g_sem.at[s, 0]),
            pltpu.make_async_copy(up0.at[:, cols], up_v.at[s], g_sem.at[s, 1]),
            pltpu.make_async_copy(wd.at[0, cols], wd_v.at[s], w_sem.at[s, 2]),
        ]

    def load(j, do):
        @pl.when(j < half_steps)
        def _():
            for c in loads(j, True):
                do(c)

        @pl.when((j >= half_steps) & (j < steps))
        def _():
            for c in loads(j, False):
                do(c)

    start, wait = (lambda c: c.start()), (lambda c: c.wait())
    slot = lax.rem(j, 2)

    def d2d(q, s):
        return pltpu.make_async_remote_copy(
            src_ref=grad_v.at[s], dst_ref=landed.at[q], send_sem=d_send.at[q], recv_sem=d_recv.at[q], device_id=beside, device_id_type=MESH)

    def exchange(k):
        return pltpu.make_async_remote_copy(
            src_ref=sums[k], dst_ref=came[k], send_sem=x_send.at[k], recv_sem=x_recv.at[k], device_id=across, device_id_type=MESH)

    def add_copy(q, s):
        return pltpu.make_async_copy(landed.at[q], add_v.at[s], add_sem.at[s])

    def ship(j):
        _, own, _, q = what(j)
        s = lax.rem(j, 2)
        pl.when(jnp.logical_not(own))(lambda: d2d(q, s).start())
        for k in range(n):
            @pl.when(own & (q == k))
            def _():
                c = pltpu.make_async_copy(grad_v.at[s], sums[k], out_sem)
                c.start()
                c.wait()
                if k < nx:
                    exchange(k).start()

    first_loads = [(a1, a_v), (dy, dy_v), (h1, b_v)]

    @pl.when(j == 0)
    def _():
        load(j, start)
        for k, (src, dst) in enumerate(first_loads):
            pltpu.make_async_copy(src, dst, in_sem.at[k]).start()
        barrier = pltpu.get_barrier_semaphore()
        for device in (beside, across):
            pl.semaphore_signal(barrier, inc=1, device_id=device, device_id_type=MESH)
        pl.semaphore_wait(barrier, 2)
        add_v[...] = jnp.zeros_like(add_v)
        for k, (src, dst) in enumerate(first_loads):
            pltpu.make_async_copy(src, dst, in_sem.at[k]).wait()

    @pl.when(j >= 2)
    def _():
        _, own, _, q = what(j - 2)
        pl.when(jnp.logical_not(own))(lambda: d2d(q, slot).wait_send())

    pl.when(j >= 1)(lambda: ship(j - 1))
    load(j, wait)
    load(j + 1, start)

    def own_at(j):
        return (j < steps) & what(j)[1]

    @pl.when(own_at(j))
    def _():
        add_copy(what(j)[3], slot).wait()

    @pl.when(jnp.logical_not(own_at(j)))
    def _():
        add_v[slot] = jnp.zeros(add_v.shape[1:], BF)

    @pl.when(own_at(j + 1))
    def _():
        q = what(j + 1)[3]
        d2d(q, slot).wait_recv()
        add_copy(q, 1 - slot).start()

    def gradients(left_a):
        for k, (left, right) in enumerate(((left_a, dg_s), (left_a, du_s), (dy_v, p_s))):
            grad_v[slot, k] = (tn(left[...], right[...]) + add_v[slot, k].astype(F32)).astype(BF)

    @pl.when(j < half_steps)
    def _():
        wgj, wuj, wdj = wg_v.at[slot], wu_v.at[slot], wd_v.at[slot]
        for r in range(t // ROWS):
            rows = pl.ds(r * ROWS, ROWS)
            a = a_v[rows]
            middle(nn(a, wgj[...]), nn(a, wuj[...]), nt(dy_v[rows], wdj[...]), rows, p_s, dg_s, du_s)
        gradients(a_v)
        for r in range(t // ROWS):
            rows = pl.ds(r * ROWS, ROWS)
            da_v[rows] = jnp.where(j == 0, 0.0, da_v[rows]) + (nt(dg_s[rows], wgj[...]) + nt(du_s[rows], wuj[...]))

    @pl.when(j == half_steps - 1)
    def _():
        def turn(r, _):
            rows = pl.ds(pl.multiple_of(r * 256, 256), 256)
            wide = b_v[rows].astype(F32)
            da = da_v[rows].astype(BF).astype(F32)
            scale = scale_of(wide)
            dot = jnp.sum(da * wide, -1, keepdims=True)
            dwide = da * scale - wide * (scale * scale * scale * dot * (1.0 / wide.shape[-1]))
            dy_v[rows] = dy_v[rows] + dwide.astype(BF)
            return 0

        lax.fori_loop(0, t // 256, turn, 0)
        c = pltpu.make_async_copy(a0, a_v, in_sem.at[0])
        c.start()
        c.wait()

    @pl.when(j >= half_steps)
    def _():
        gj, uj, wdj = gate_v.at[slot], up_v.at[slot], wd_v.at[slot]
        for r in range(t // ROWS):
            rows = pl.ds(r * ROWS, ROWS)
            middle(gj[rows], uj[rows], nt(dy_v[rows], wdj[...]), rows, p_s, dg_s, du_s)
        gradients(a_v)

    @pl.when(j == steps - 1)
    def _():
        ship(j)
        for k in range(nx):
            exchange(k).wait()

def both(a1, h1, dy, a0, weights, saved, nx):
    t, d = a1.shape
    ff = weights[2].shape[1]
    n = 2 * (ff // 2 // CHUNK)
    anywhere = pl.BlockSpec(memory_space=pl.ANY)
    chunk = jax.ShapeDtypeStruct((3, d, CHUNK), BF)
    outs = [chunk] * (n + nx) + [jax.ShapeDtypeStruct((n, 3, d, CHUNK), BF)]
    out = pl.pallas_call(
        functools.partial(both_kernel, nx),
        grid=(2 * n,),
        in_specs=[anywhere] * 9,
        out_specs=[anywhere] * len(outs),
        out_shape=outs,
        scratch_shapes=[pltpu.VMEM((t, d), BF)] * 3 + [pltpu.VMEM((t, d), F32)] + [pltpu.VMEM((t, CHUNK), BF)] * 3
        + [pltpu.VMEM((2, d, CHUNK), BF)] * 2 + [pltpu.VMEM((2, CHUNK, d), BF)] + [pltpu.VMEM((2, t, CHUNK), F32)] * 2
        + [pltpu.VMEM((2, 3, d, CHUNK), BF)] * 2
        + [pltpu.SemaphoreType.DMA((3,)), pltpu.SemaphoreType.DMA((2, 3)), pltpu.SemaphoreType.DMA((2, 2)), pltpu.SemaphoreType.DMA((2,)), pltpu.SemaphoreType.DMA]
        + [pltpu.SemaphoreType.DMA((n,))] * 2 + [pltpu.SemaphoreType.DMA((max(nx, 1),))] * 2,
        compiler_params=pltpu.CompilerParams(vmem_limit_bytes=67_000_000, collective_id=1, has_side_effects=True),
        cost_estimate=pl.CostEstimate(flops=24 * t * d * ff, bytes_accessed=8 * t * ff, transcendentals=0),
        name="backward",
    )(a1, h1, dy, a0, *weights, *saved)
    return out[:n], out[n : n + nx]


def adamw_kernel(own, aliased, chunks, off_ref, *refs):
    gs, refs = refs[: (1 + own) * chunks], refs[(1 + own) * chunks :]
    w, m, v = refs[0:3], refs[3:6], refs[6:9]
    refs = refs[9 + 9 * aliased :]
    new_w, new_m, new_v = refs[0:3], refs[3:6], refs[6:9]

    def work(g_refs):
        for i in range(3):
            g = g_refs[0][i].astype(F32)
            if own:
                total = (g + g_refs[1][i].astype(F32)).astype(BF)
                refs[9][i] = total
                g = total.astype(F32)
            if i == 2:
                g = g.T
            mi = 0.9 * m[i][...] + 0.1 * g
            vi = 0.95 * v[i][...] + 0.05 * g * g
            wi = w[i][...].astype(F32)
            step = mi * lax.rsqrt(vi + 1e-8) + 0.1 * wi
            new_w[i][...] = (wi - 0.02 * step).astype(BF)
            new_m[i][...] = mi
            new_v[i][...] = vi

    per = CHUNK // ADAM_COLS
    for k in range(chunks if own else 1):
        g_refs = gs[k * (1 + own) : (k + 1) * (1 + own)]
        if own and chunks > 1:
            pl.when(pl.program_id(0) // per == k)(functools.partial(work, g_refs))
        else:
            work(g_refs)


def adamw(off, gs, weights, m, v, new, layer, own):
    d, unit = gs[0].shape[1:]
    chunks = len(gs) // 2 if own else 1
    unit *= chunks
    per = CHUNK // ADAM_COLS
    wide = pl.BlockSpec((None, d, ADAM_COLS), lambda j, o: (layer, 0, o[0] + j))
    tall = pl.BlockSpec((None, ADAM_COLS, d), lambda j, o: (layer, o[0] + j, 0))
    grad = pl.BlockSpec((3, d, ADAM_COLS), lambda j, o: (0, 0, j))

    def part(k):
        return pl.BlockSpec((3, d, ADAM_COLS), lambda j, o: (0, 0, jnp.clip(j - k * per, 0, per - 1)))

    kinds = [wide, wide, tall] * 3
    shapes = [jax.ShapeDtypeStruct(x.shape, x.dtype) for x in (*weights, *m, *v)]
    out = pl.pallas_call(
        functools.partial(adamw_kernel, own, new is not None, chunks),
        grid_spec=pltpu.PrefetchScalarGridSpec(
            num_scalar_prefetch=1,
            grid=(unit // ADAM_COLS,),
            in_specs=([part(k // 2) for k in range(2 * chunks)] if own else [grad])
            + kinds
            + ([pl.BlockSpec(memory_space=pl.ANY)] * 9 if new is not None else []),
            out_specs=kinds + [grad] * own,
        ),
        out_shape=shapes + [jax.ShapeDtypeStruct((3, d, unit), BF)] * own,
        input_output_aliases={10 + len(gs) + i: i for i in range(9)} if new is not None else {},
        compiler_params=pltpu.CompilerParams(vmem_limit_bytes=VMEM),
        cost_estimate=pl.CostEstimate(flops=int(8 * 3 * d * unit * 30), bytes_accessed=22 * 3 * d * unit, transcendentals=0),
        name="adamw_own" if own else "adamw_other",
    )(off, *gs, *weights, *m, *v, *(new or ()))
    return out[:9], out[9:]


ORDER = (
    "F", "G", "x5", "x6", "A0+1", "h0", "A2+3", "h2", "B0+1", "x7", "B2+3", "x8",
    "A4", "h4", "A5", "h5", "B4", "x9", "B5", "x10", "A6+7", "h6", "x11", "B6+7",
    "A8", "h8", "A9", "h9", "B8", "B9", "A10", "h10", "A11", "h11", "B10", "B11",
)


def chunks_of(name):
    first, *more = name[1:].split("+")
    return range(int(first), 1 + int(more[0] if more else first))


def solution(mesh):
    reps, dps = mesh.shape["rep"], mesh.shape["dp"]

    def pairs(to):
        return [(r * dps + i, r * dps + to(i)) for r in range(reps) for i in range(dps)]

    across = pairs(lambda i: (i + 2) % dps)
    beside = pairs(lambda i: i ^ 1)

    def step(x, dy, *arrays):
        weights, m, v = (arrays[i : i + 3] for i in (0, 3, 6))
        core = lax.axis_index("dp") % 2
        half = weights[0].shape[2] // 2
        per = half // CHUNK
        have = {}
        new = None

        def offset(side, number):
            return ((side * half + number * CHUNK) // ADAM_COLS).astype(jnp.int32).reshape(1)

        def send(z, to):
            return lax.ppermute(z, AXES, to)

        for name in ORDER:
            kind = name[0]
            if kind == "F":
                h1, a0, a1, gate0, up0 = forward(x[0], *weights, 0)
            elif kind == "G":
                sums, came = both(a1, h1, dy[0], a0, weights, (gate0, up0), NX)
                came = list(came) + [None] * (2 * per - NX)
            elif kind == "x":
                k = int(name[1:])
                came[k] = send(sums[k], across)
            elif kind == "h":
                have[name[1:]] = send(have["A" + name[1:]], beside)
            else:
                ks = chunks_of(name)
                layer, number, first = 1 - ks[0] // per, ks[0] % per, str(ks[0])
                if kind == "A":
                    gs = [z for k in ks for z in (sums[k], came[k])]
                    new, (have["A" + first],) = adamw(offset(core, number), gs, weights, m, v, new, layer, 1)
                else:
                    new, _ = adamw(offset(1 - core, number), [have[first]], weights, m, v, new, layer, 0)
        return tuple(new)

    return jax.shard_map(
        step,
        mesh=mesh,
        in_specs=(P(("rep", "dp"), None, None),) * 2 + (P(None, None, None),) * 9,
        out_specs=(P("rep", None, None),) * 9,
        check_vma=False,
    )
```

time: 1680 us -> 906 us (0.54)
  waiting for transfers between devices: 926 us -> 225 us
  Pallas kernels: 0 us -> 664 us
  matrix products: 521 us -> 0 us
  other arithmetic: 206 us -> 0 us
    psum x1 -> x0, waiting for transfers between devices: 926 us -> none  [step(): summed[number] = [lax.psum(by_w[name], 'dp') for name in NAMES]]
    pallas_call x0 -> x20, Pallas kernels: none -> 664 us  [the longest x1 326 us: both(): pl.pallas_call(functools.partial(both_kernel, nx), grid=(2 * n,), in_spec...]
    dot_general x15 -> x0, matrix products: 521 us -> none  [the longest x5 194 us: layer(): gate = jnp.dot(a, w['w_gate'], preferred_element_type=jnp.float32)]
    ppermute x0 -> x16, waiting for transfers between devices: none -> 225 us  [send(): return lax.ppermute(z, AXES, to)]
    convert_element_type x2 -> x0, other arithmetic: 200 us -> none  [adamw(): return ((w - 0.02 * step).astype(jnp.bfloat16), m, v)]
  transfers between devices with their start and end apart: 1 -> 16, of which waited for: 1 -> 8; matrix products, arithmetic and copies ran while one was open for 0% -> 0% of each run, Pallas kernels for 0% -> 23%
where the time goes in v1:
time: 906 us; the launch traced here: 900 us
  Pallas kernels  664 us (73%)
  waiting for transfers between devices  225 us (25%)
  starting transfers between devices  10.2 us (1%)
    pallas_call x1, Pallas kernels, both(): pl.pallas_call(functools.partial(both_kernel, nx), grid=(2 * n,), in_spec...  326 us
    pallas_call x18, Pallas kernels, adamw(): pl.pallas_call(functools.partial(adamw_kernel, own, new is not None, chun...  262 us
    ppermute x16, waiting for transfers between devices, send(): return lax.ppermute(z, AXES, to)  225 us
    pallas_call x1, Pallas kernels, forward(): pl.pallas_call(functools.partial(forward_kernel, rows), grid=(ff // chunk...  76.1 us
  transfers between devices with their start and end apart: 16, of which 8 were waited for; matrix products, arithmetic and copies ran while one was open for 0% of the time, Pallas kernels for 23%

profile of v1, /device:TPU:0, one launch (start us, length us, event | category | flops | bytes accessed | tf_op | source)
XLA Modules:
  0.0 900.1 jit_solution(8538641915357476576)
XLA Ops:
  0.7 76.1 %forward.1 = (bf16[2048,768]{1,0:T(8,128)(2,1)}, bf16[2048,768]{1,0:T(8,128)(2,1)}, bf16[2048,768]{1,0:T(8,128)(2,1)}, f32[2048,6144]{1,0:T(8,128)}, f32[2048,6144]{1,0:T(8,128)}) custom-call(bf16[2048,768]{1,0:T(8,128)(2,1)} %bitcast.12, bf16[2,768,6144]{2,1,0:T(8,128)(2,1)} %refs_1_.17, bf16[2,768,6144]{2,1,0:T(8,128)(2,1)} %refs_2_.29, ...), custom_call_target="tpu_custom_call" | custom-call | flops 57982058496 | bytes 100663296 | tf_op jit(solution)/shard_map/forward/pallas_call | solution.py:70
  76.8 326.0 %backward.1 = (bf16[3,768,512]{2,1,0:T(8,128)(2,1)}, bf16[3,768,512]{2,1,0:T(8,128)(2,1)}, bf16[3,768,512]{2,1,0:T(8,128)(2,1)}, bf16[3,768,512]{2,1,0:T(8,128)(...) custom-call(bf16[2048,768]{1,0:T(8,128)(2,1)} %get-tuple-element.193, ...), custom_call_target="tpu_custom_call" | custom-call | flops 231928233984 | bytes 100663296 | tf_op jit(solution)/shard_map/backward/pallas_call | solution.py:268
  402.7 23.8 %adamw_own.9 = (bf16[2,768,6144]{2,1,0:T(8,128)(2,1)}, bf16[2,768,6144]{2,1,0:T(8,128)(2,1)}, bf16[2,6144,768]{2,1,0:T(8,128)(2,1)}, f32[2,768,6144]{2,1,0:T(8,1...) custom-call(s32[1]{0:T(128)} %bitcast.9.off_ref, ...), custom_call_target="tpu_custom_call" | custom-call | flops 566231040 | bytes 51904512 | tf_op jit(solution)/shard_map/adamw_own/pallas_call | solution.py:332
  426.6 0.6 collective-permute-start.8
  427.2 23.6 %adamw_own.10 = (bf16[2,768,6144]{2,1,0:T(8,128)(2,1)}, bf16[2,768,6144]{2,1,0:T(8,128)(2,1)}, bf16[2,6144,768]{2,1,0:T(8,128)(2,1)}, f32[2,768,6144]{2,1,0:T(8,...) custom-call(s32[1]{0:T(128)} %bitcast.7.off_ref, ...), custom_call_target="tpu_custom_call", output_to_operand_aliasing={{0}: (14, {}), {1}: (15, {}), {2}: (16, {}), {3}: (17, {}),... | custom-call | flops 566231040 | bytes 51904512 | tf_op jit(solution)/shard_map/adamw_own/pallas_call | solution.py:332
  450.8 0.1 collective-permute-start.7
  451.0 3.1 collective-permute-start.6
  454.1 0.0 collective-permute-done.8.refs_0_
  454.1 18.8 %adamw_other.9 = (bf16[2,768,6144]{2,1,0:T(8,128)(2,1)}, bf16[2,768,6144]{2,1,0:T(8,128)(2,1)}, bf16[2,6144,768]{2,1,0:T(8,128)(2,1)}, f32[2,768,6144]{2,1,0:T(8...) custom-call(s32[1]{0:T(128)} %bitcast.8.off_ref, ...), custom_call_target="tpu_custom_call", output_to_operand_aliasing={{0}: (11, {}), {1}: (12, {}), {2}: (13, {}), {3}: (14, {}),... | custom-call | flops 566231040 | bytes 51904512 | tf_op jit(solution)/shard_map/adamw_other/pallas_call | solution.py:332
  472.9 0.0 collective-permute-done.7.refs_0_
  472.9 19.0 %adamw_other.10 = (bf16[2,768,6144]{2,1,0:T(8,128)(2,1)}, bf16[2,768,6144]{2,1,0:T(8,128)(2,1)}, bf16[2,6144,768]{2,1,0:T(8,128)(2,1)}, f32[2,768,6144]{2,1,0:T(...) custom-call(s32[1]{0:T(128)} %bitcast.10.off_ref, ...), custom_call_target="tpu_custom_call", output_to_operand_aliasing={{0}: (11, {}), {1}: (12, {}), {2}: (13, {}), {3}: (14, {}),... | custom-call | flops 566231040 | bytes 51904512 | tf_op jit(solution)/shard_map/adamw_other/pallas_call | solution.py:332
  491.9 11.9 %adamw_own.11 = (bf16[2,768,6144]{2,1,0:T(8,128)(2,1)}, bf16[2,768,6144]{2,1,0:T(8,128)(2,1)}, bf16[2,6144,768]{2,1,0:T(8,128)(2,1)}, f32[2,768,6144]{2,1,0:T(8,...) custom-call(s32[1]{0:T(128)} %bitcast.4.off_ref, ...), custom_call_target="tpu_custom_call", output_to_operand_aliasing={{0}: (12, {}), {1}: (13, {}), {2}: (14, {}), {3}: (15, {}),... | custom-call | flops 283115520 | bytes 25952256 | tf_op jit(solution)/shard_map/adamw_own/pallas_call | solution.py:332
  503.8 0.0 collective-permute-start.10
  503.8 2.0 collective-permute-done.6.refs_1_
  505.9 11.8 %adamw_own.12 = (bf16[2,768,6144]{2,1,0:T(8,128)(2,1)}, bf16[2,768,6144]{2,1,0:T(8,128)(2,1)}, bf16[2,6144,768]{2,1,0:T(8,128)(2,1)}, f32[2,768,6144]{2,1,0:T(8,...) custom-call(s32[1]{0:T(128)} %bitcast.1.off_ref, ...), custom_call_target="tpu_custom_call", output_to_operand_aliasing={{0}: (12, {}), {1}: (13, {}), {2}: (14, {}), {3}: (15, {}),... | custom-call | flops 283115520 | bytes 25952256 | tf_op jit(solution)/shard_map/adamw_own/pallas_call | solution.py:332
  517.7 0.0 collective-permute-start.9
  517.8 1.8 collective-permute-start.4
  519.5 0.3 collective-permute-start.5
  519.8 0.0 collective-permute-done.10.refs_0_
  519.8 10.7 %adamw_other.11 = (bf16[2,768,6144]{2,1,0:T(8,128)(2,1)}, bf16[2,768,6144]{2,1,0:T(8,128)(2,1)}, bf16[2,6144,768]{2,1,0:T(8,128)(2,1)}, f32[2,768,6144]{2,1,0:T(...) custom-call(s32[1]{0:T(128)} %bitcast.11.off_ref, ...), custom_call_target="tpu_custom_call", output_to_operand_aliasing={{0}: (11, {}), {1}: (12, {}), {2}: (13, {}), {3}: (14, {}),... | custom-call | flops 283115520 | bytes 25952256 | tf_op jit(solution)/shard_map/adamw_other/pallas_call | solution.py:332
  530.5 0.0 collective-permute-done.9.refs_0_
  530.5 10.3 %adamw_other.12 = (bf16[2,768,6144]{2,1,0:T(8,128)(2,1)}, bf16[2,768,6144]{2,1,0:T(8,128)(2,1)}, bf16[2,6144,768]{2,1,0:T(8,128)(2,1)}, f32[2,768,6144]{2,1,0:T(...) custom-call(s32[1]{0:T(128)} %bitcast.off_ref, ...), custom_call_target="tpu_custom_call", output_to_operand_aliasing={{0}: (11, {}), {1}: (12, {}), {2}: (13, {}), {3}: (14, {}),... | custom-call | flops 283115520 | bytes 25952256 | tf_op jit(solution)/shard_map/adamw_other/pallas_call | solution.py:332
  540.8 31.5 %collective-permute-done.4.refs_1_ = bf16[3,768,512]{2,1,0:T(8,128)(2,1)} collective-permute-done((bf16[3,768,512]{2,1,0:T(8,128)(2,1)}, bf16[3,768,512]{2,1,0:T(8,128)(2,1)}, u32[]{:S(2)}, u32[]{:S(2)}) %collective-permute-start.4) | collective-permute-done | bytes 2359328 | tf_op jit(solution)/shard_map/ppermute | solution.py:384
  572.2 50.1 %collective-permute-done.5.refs_3_ = bf16[3,768,512]{2,1,0:T(8,128)(2,1)} collective-permute-done((bf16[3,768,512]{2,1,0:T(8,128)(2,1)}, bf16[3,768,512]{2,1,0:T(8,128)(2,1)}, u32[]{:S(2)}, u32[]{:S(2)}) %collective-permute-start.5) | collective-permute-done | bytes 2359328 | tf_op jit(solution)/shard_map/ppermute | solution.py:384
  622.3 23.9 %adamw_own.13 = (bf16[2,768,6144]{2,1,0:T(8,128)(2,1)}, bf16[2,768,6144]{2,1,0:T(8,128)(2,1)}, bf16[2,6144,768]{2,1,0:T(8,128)(2,1)}, f32[2,768,6144]{2,1,0:T(8,...) custom-call(s32[1]{0:T(128)} %bitcast.9.off_ref, ...), custom_call_target="tpu_custom_call", output_to_operand_aliasing={{0}: (14, {}), {1}: (15, {}), {2}: (16, {}), {3}: (17, {}),... | custom-call | flops 566231040 | bytes 51904512 | tf_op jit(solution)/shard_map/adamw_own/pallas_call | solution.py:332
  646.2 0.0 collective-permute-start.11
  646.3 1.8 collective-permute-start.3
  648.0 0.3 collective-permute-start.2
  648.3 6.2 collective-permute-done.11.refs_0_
  654.5 18.8 %adamw_other.13 = (bf16[2,768,6144]{2,1,0:T(8,128)(2,1)}, bf16[2,768,6144]{2,1,0:T(8,128)(2,1)}, bf16[2,6144,768]{2,1,0:T(8,128)(2,1)}, f32[2,768,6144]{2,1,0:T(...) custom-call(s32[1]{0:T(128)} %bitcast.8.off_ref, ...), custom_call_target="tpu_custom_call", output_to_operand_aliasing={{0}: (11, {}), {1}: (12, {}), {2}: (13, {}), {3}: (14, {}),... | custom-call | flops 566231040 | bytes 51904512 | tf_op jit(solution)/shard_map/adamw_other/pallas_call | solution.py:332
  673.3 27.4 %collective-permute-done.3.refs_1_ = bf16[3,768,512]{2,1,0:T(8,128)(2,1)} collective-permute-done((bf16[3,768,512]{2,1,0:T(8,128)(2,1)}, bf16[3,768,512]{2,1,0:T(8,128)(2,1)}, u32[]{:S(2)}, u32[]{:S(2)}) %collective-permute-start.3) | collective-permute-done | bytes 2359328 | tf_op jit(solution)/shard_map/ppermute | solution.py:384
  700.7 12.0 %adamw_own.14 = (bf16[2,768,6144]{2,1,0:T(8,128)(2,1)}, bf16[2,768,6144]{2,1,0:T(8,128)(2,1)}, bf16[2,6144,768]{2,1,0:T(8,128)(2,1)}, f32[2,768,6144]{2,1,0:T(8,...) custom-call(s32[1]{0:T(128)} %bitcast.7.off_ref, ...), custom_call_target="tpu_custom_call", output_to_operand_aliasing={{0}: (12, {}), {1}: (13, {}), {2}: (14, {}), {3}: (15, {}),... | custom-call | flops 283115520 | bytes 25952256 | tf_op jit(solution)/shard_map/adamw_own/pallas_call | solution.py:332
  712.8 0.0 collective-permute-start.13
  712.8 38.0 %collective-permute-done.2.refs_1_ = bf16[3,768,512]{2,1,0:T(8,128)(2,1)} collective-permute-done((bf16[3,768,512]{2,1,0:T(8,128)(2,1)}, bf16[3,768,512]{2,1,0:T(8,128)(2,1)}, u32[]{:S(2)}, u32[]{:S(2)}) %collective-permute-start.2) | collective-permute-done | bytes 2359328 | tf_op jit(solution)/shard_map/ppermute | solution.py:384
  750.8 11.8 %adamw_own.15 = (bf16[2,768,6144]{2,1,0:T(8,128)(2,1)}, bf16[2,768,6144]{2,1,0:T(8,128)(2,1)}, bf16[2,6144,768]{2,1,0:T(8,128)(2,1)}, f32[2,768,6144]{2,1,0:T(8,...) custom-call(s32[1]{0:T(128)} %bitcast.6.off_ref, ...), custom_call_target="tpu_custom_call", output_to_operand_aliasing={{0}: (12, {}), {1}: (13, {}), {2}: (14, {}), {3}: (15, {}),... | custom-call | flops 283115520 | bytes 25952256 | tf_op jit(solution)/shard_map/adamw_own/pallas_call | solution.py:332
  762.6 0.0 collective-permute-start.12
  762.7 1.8 collective-permute-start.1
  764.4 0.3 collective-permute-start
  764.7 0.0 collective-permute-done.13.refs_0_
  764.7 10.2 %adamw_other.14 = (bf16[2,768,6144]{2,1,0:T(8,128)(2,1)}, bf16[2,768,6144]{2,1,0:T(8,128)(2,1)}, bf16[2,6144,768]{2,1,0:T(8,128)(2,1)}, f32[2,768,6144]{2,1,0:T(...) custom-call(s32[1]{0:T(128)} %bitcast.10.off_ref, ...), custom_call_target="tpu_custom_call", output_to_operand_aliasing={{0}: (11, {}), {1}: (12, {}), {2}: (13, {}), {3}: (14, {}),... | custom-call | flops 283115520 | bytes 25952256 | tf_op jit(solution)/shard_map/adamw_other/pallas_call | solution.py:332
  775.0 0.0 collective-permute-done.12.refs_0_
  775.0 10.8 %adamw_other.15 = (bf16[2,768,6144]{2,1,0:T(8,128)(2,1)}, bf16[2,768,6144]{2,1,0:T(8,128)(2,1)}, bf16[2,6144,768]{2,1,0:T(8,128)(2,1)}, f32[2,768,6144]{2,1,0:T(...) custom-call(s32[1]{0:T(128)} %bitcast.5.off_ref, ...), custom_call_target="tpu_custom_call", output_to_operand_aliasing={{0}: (11, {}), {1}: (12, {}), {2}: (13, {}), {3}: (14, {}),... | custom-call | flops 283115520 | bytes 25952256 | tf_op jit(solution)/shard_map/adamw_other/pallas_call | solution.py:332
  785.8 31.4 %collective-permute-done.1.refs_1_ = bf16[3,768,512]{2,1,0:T(8,128)(2,1)} collective-permute-done((bf16[3,768,512]{2,1,0:T(8,128)(2,1)}, bf16[3,768,512]{2,1,0:T(8,128)(2,1)}, u32[]{:S(2)}, u32[]{:S(2)}) %collective-permute-start.1) | collective-permute-done | bytes 2359328 | tf_op jit(solution)/shard_map/ppermute | solution.py:384
  817.1 11.9 %adamw_own.16 = (bf16[2,768,6144]{2,1,0:T(8,128)(2,1)}, bf16[2,768,6144]{2,1,0:T(8,128)(2,1)}, bf16[2,6144,768]{2,1,0:T(8,128)(2,1)}, f32[2,768,6144]{2,1,0:T(8,...) custom-call(s32[1]{0:T(128)} %bitcast.4.off_ref, ...), custom_call_target="tpu_custom_call", output_to_operand_aliasing={{0}: (12, {}), {1}: (13, {}), {2}: (14, {}), {3}: (15, {}),... | custom-call | flops 283115520 | bytes 25952256 | tf_op jit(solution)/shard_map/adamw_own/pallas_call | solution.py:332
  829.0 0.0 collective-permute-start.15
  829.0 38.2 %collective-permute-done.refs_1_ = bf16[3,768,512]{2,1,0:T(8,128)(2,1)} collective-permute-done((bf16[3,768,512]{2,1,0:T(8,128)(2,1)}, bf16[3,768,512]{2,1,0:T(8,128)(2,1)}, u32[]{:S(2)}, u32[]{:S(2)}) %collective-permute-start) | collective-permute-done | bytes 2359328 | tf_op jit(solution)/shard_map/ppermute | solution.py:384
  867.2 11.9 %adamw_own.17 = (bf16[2,768,6144]{2,1,0:T(8,128)(2,1)}, bf16[2,768,6144]{2,1,0:T(8,128)(2,1)}, bf16[2,6144,768]{2,1,0:T(8,128)(2,1)}, f32[2,768,6144]{2,1,0:T(8,...) custom-call(s32[1]{0:T(128)} %bitcast.1.off_ref, ...), custom_call_target="tpu_custom_call", output_to_operand_aliasing={{0}: (12, {}), {1}: (13, {}), {2}: (14, {}), {3}: (15, {}),... | custom-call | flops 283115520 | bytes 25952256 | tf_op jit(solution)/shard_map/adamw_own/pallas_call | solution.py:332
  879.0 0.0 collective-permute-start.14
  879.1 0.0 collective-permute-done.15.refs_0_
  879.1 10.5 %adamw_other.16 = (bf16[2,768,6144]{2,1,0:T(8,128)(2,1)}, bf16[2,768,6144]{2,1,0:T(8,128)(2,1)}, bf16[2,6144,768]{2,1,0:T(8,128)(2,1)}, f32[2,768,6144]{2,1,0:T(...) custom-call(s32[1]{0:T(128)} %bitcast.11.off_ref, ...), custom_call_target="tpu_custom_call", output_to_operand_aliasing={{0}: (11, {}), {1}: (12, {}), {2}: (13, {}), {3}: (14, {}),... | custom-call | flops 283115520 | bytes 25952256 | tf_op jit(solution)/shard_map/adamw_other/pallas_call | solution.py:332
  889.6 0.0 collective-permute-done.14.refs_0_
  889.6 10.4 %adamw_other.17 = (bf16[2,768,6144]{2,1,0:T(8,128)(2,1)}, bf16[2,768,6144]{2,1,0:T(8,128)(2,1)}, bf16[2,6144,768]{2,1,0:T(8,128)(2,1)}, f32[2,768,6144]{2,1,0:T(...) custom-call(s32[1]{0:T(128)} %bitcast.off_ref, ...), custom_call_target="tpu_custom_call", output_to_operand_aliasing={{0}: (11, {}), {1}: (12, {}), {2}: (13, {}), {3}: (14, {}),... | custom-call | flops 283115520 | bytes 25952256 | tf_op jit(solution)/shard_map/adamw_other/pallas_call | solution.py:332
Async XLA Ops:
  426.6 27.5 %collective-permute-start.8 = (bf16[3,768,1024]{2,1,0:T(8,128)(2,1)}, bf16[3,768,1024]{2,1,0:T(8,128)(2,1)}, u32[]{:S(2)}, u32[]{:S(2)}) collective-permute-start(bf16[3,768,1024]{2,1,0:T(8,128)(2,1)} %get-tuple-element.225), channel_id=1, source_target_pairs={{0,1},{1,0},{2,3},{3,2},{4,5},{5,4},{6,7},{7,6}} | collective-permute-start | bytes 14155784 | tf_op jit(solution)/shard_map/ppermute | solution.py:384
  450.8 22.0 %collective-permute-start.7 = (bf16[3,768,1024]{2,1,0:T(8,128)(2,1)}, bf16[3,768,1024]{2,1,0:T(8,128)(2,1)}, u32[]{:S(2)}, u32[]{:S(2)}) collective-permute-start(bf16[3,768,1024]{2,1,0:T(8,128)(2,1)} %get-tuple-element.224), channel_id=1, source_target_pairs={{0,1},{1,0},{2,3},{3,2},{4,5},{5,4},{6,7},{7,6}} | collective-permute-start | bytes 14155784 | tf_op jit(solution)/shard_map/ppermute | solution.py:384
  451.0 54.9 %collective-permute-start.6 = (bf16[3,768,512]{2,1,0:T(8,128)(2,1)}, bf16[3,768,512]{2,1,0:T(8,128)(2,1)}, u32[]{:S(2)}, u32[]{:S(2)}) collective-permute-start(bf16[3,768,512]{2,1,0:T(8,128)(2,1)} %get-tuple-element.204.refs_0_), channel_id=1, source_target_pairs={{0,2},{1,3},{2,0},{3,1},{4,6},{5,7},{6,4},{7,5}} | collective-permute-start | bytes 7077896 | tf_op jit(solution)/shard_map/ppermute | solution.py:384
  503.8 16.0 %collective-permute-start.10 = (bf16[3,768,512]{2,1,0:T(8,128)(2,1)}, bf16[3,768,512]{2,1,0:T(8,128)(2,1)}, u32[]{:S(2)}, u32[]{:S(2)}) collective-permute-start(bf16[3,768,512]{2,1,0:T(8,128)(2,1)} %get-tuple-element.263), channel_id=1, source_target_pairs={{0,1},{1,0},{2,3},{3,2},{4,5},{5,4},{6,7},{7,6}} | collective-permute-start | bytes 7077896 | tf_op jit(solution)/shard_map/ppermute | solution.py:384
  517.7 12.7 %collective-permute-start.9 = (bf16[3,768,512]{2,1,0:T(8,128)(2,1)}, bf16[3,768,512]{2,1,0:T(8,128)(2,1)}, u32[]{:S(2)}, u32[]{:S(2)}) collective-permute-start(bf16[3,768,512]{2,1,0:T(8,128)(2,1)} %get-tuple-element.262), channel_id=1, source_target_pairs={{0,1},{1,0},{2,3},{3,2},{4,5},{5,4},{6,7},{7,6}} | collective-permute-start | bytes 7077896 | tf_op jit(solution)/shard_map/ppermute | solution.py:384
  517.8 54.5 %collective-permute-start.4 = (bf16[3,768,512]{2,1,0:T(8,128)(2,1)}, bf16[3,768,512]{2,1,0:T(8,128)(2,1)}, u32[]{:S(2)}, u32[]{:S(2)}) collective-permute-start(bf16[3,768,512]{2,1,0:T(8,128)(2,1)} %get-tuple-element.202.refs_0_), channel_id=1, source_target_pairs={{0,2},{1,3},{2,0},{3,1},{4,6},{5,7},{6,4},{7,5}} | collective-permute-start | bytes 7077896 | tf_op jit(solution)/shard_map/ppermute | solution.py:384
  519.5 102.8 %collective-permute-start.5 = (bf16[3,768,512]{2,1,0:T(8,128)(2,1)}, bf16[3,768,512]{2,1,0:T(8,128)(2,1)}, u32[]{:S(2)}, u32[]{:S(2)}) collective-permute-start(bf16[3,768,512]{2,1,0:T(8,128)(2,1)} %get-tuple-element.203.refs_2_), channel_id=1, source_target_pairs={{0,2},{1,3},{2,0},{3,1},{4,6},{5,7},{6,4},{7,5}} | collective-permute-start | bytes 7077896 | tf_op jit(solution)/shard_map/ppermute | solution.py:384
  646.2 8.3 collective-permute-start.11
  646.3 54.5 %collective-permute-start.3 = (bf16[3,768,512]{2,1,0:T(8,128)(2,1)}, bf16[3,768,512]{2,1,0:T(8,128)(2,1)}, u32[]{:S(2)}, u32[]{:S(2)}) collective-permute-start(bf16[3,768,512]{2,1,0:T(8,128)(2,1)} %get-tuple-element.201.refs_0_), channel_id=1, source_target_pairs={{0,2},{1,3},{2,0},{3,1},{4,6},{5,7},{6,4},{7,5}} | collective-permute-start | bytes 7077896 | tf_op jit(solution)/shard_map/ppermute | solution.py:384
  648.0 102.8 %collective-permute-start.2 = (bf16[3,768,512]{2,1,0:T(8,128)(2,1)}, bf16[3,768,512]{2,1,0:T(8,128)(2,1)}, u32[]{:S(2)}, u32[]{:S(2)}) collective-permute-start(bf16[3,768,512]{2,1,0:T(8,128)(2,1)} %get-tuple-element.200.refs_0_), channel_id=1, source_target_pairs={{0,2},{1,3},{2,0},{3,1},{4,6},{5,7},{6,4},{7,5}} | collective-permute-start | bytes 7077896 | tf_op jit(solution)/shard_map/ppermute | solution.py:384
  712.8 51.9 %collective-permute-start.13 = (bf16[3,768,512]{2,1,0:T(8,128)(2,1)}, bf16[3,768,512]{2,1,0:T(8,128)(2,1)}, u32[]{:S(2)}, u32[]{:S(2)}) collective-permute-start(bf16[3,768,512]{2,1,0:T(8,128)(2,1)} %get-tuple-element.320), channel_id=1, source_target_pairs={{0,1},{1,0},{2,3},{3,2},{4,5},{5,4},{6,7},{7,6}} | collective-permute-start | bytes 7077896 | tf_op jit(solution)/shard_map/ppermute | solution.py:384
  762.6 12.3 %collective-permute-start.12 = (bf16[3,768,512]{2,1,0:T(8,128)(2,1)}, bf16[3,768,512]{2,1,0:T(8,128)(2,1)}, u32[]{:S(2)}, u32[]{:S(2)}) collective-permute-start(bf16[3,768,512]{2,1,0:T(8,128)(2,1)} %get-tuple-element.319), channel_id=1, source_target_pairs={{0,1},{1,0},{2,3},{3,2},{4,5},{5,4},{6,7},{7,6}} | collective-permute-start | bytes 7077896 | tf_op jit(solution)/shard_map/ppermute | solution.py:384
  762.7 54.5 %collective-permute-start.1 = (bf16[3,768,512]{2,1,0:T(8,128)(2,1)}, bf16[3,768,512]{2,1,0:T(8,128)(2,1)}, u32[]{:S(2)}, u32[]{:S(2)}) collective-permute-start(bf16[3,768,512]{2,1,0:T(8,128)(2,1)} %get-tuple-element.199.refs_0_), channel_id=1, source_target_pairs={{0,2},{1,3},{2,0},{3,1},{4,6},{5,7},{6,4},{7,5}} | collective-permute-start | bytes 7077896 | tf_op jit(solution)/shard_map/ppermute | solution.py:384
  764.4 102.8 %collective-permute-start = (bf16[3,768,512]{2,1,0:T(8,128)(2,1)}, bf16[3,768,512]{2,1,0:T(8,128)(2,1)}, u32[]{:S(2)}, u32[]{:S(2)}) collective-permute-start(bf16[3,768,512]{2,1,0:T(8,128)(2,1)} %get-tuple-element.198.refs_0_), channel_id=1, source_target_pairs={{0,2},{1,3},{2,0},{3,1},{4,6},{5,7},{6,4},{7,5}} | collective-permute-start | bytes 7077896 | tf_op jit(solution)/shard_map/ppermute | solution.py:384
  829.0 50.1 %collective-permute-start.15 = (bf16[3,768,512]{2,1,0:T(8,128)(2,1)}, bf16[3,768,512]{2,1,0:T(8,128)(2,1)}, u32[]{:S(2)}, u32[]{:S(2)}) collective-permute-start(bf16[3,768,512]{2,1,0:T(8,128)(2,1)} %get-tuple-element.358), channel_id=1, source_target_pairs={{0,1},{1,0},{2,3},{3,2},{4,5},{5,4},{6,7},{7,6}} | collective-permute-start | bytes 7077896 | tf_op jit(solution)/shard_map/ppermute | solution.py:384
  879.0 10.5 %collective-permute-start.14 = (bf16[3,768,512]{2,1,0:T(8,128)(2,1)}, bf16[3,768,512]{2,1,0:T(8,128)(2,1)}, u32[]{:S(2)}, u32[]{:S(2)}) collective-permute-start(bf16[3,768,512]{2,1,0:T(8,128)(2,1)} %get-tuple-element.357), channel_id=1, source_target_pairs={{0,1},{1,0},{2,3},{3,2},{4,5},{5,4},{6,7},{7,6}} | collective-permute-start | bytes 7077896 | tf_op jit(solution)/shard_map/ppermute | solution.py:384

commit v2 on v1

v2 whole, which is shorter than its diff:
```python
import functools

import jax
import jax.numpy as jnp
from jax import lax
from jax.experimental import pallas as pl
from jax.experimental.pallas import tpu as pltpu
from jax.sharding import PartitionSpec as P


BF, F32 = jnp.bfloat16, jnp.float32
AXES = ("rep", "dp")
MESH = pl.DeviceIdType.MESH
CHUNK = 512
ROWS = 512
ADAM_COLS = 256
VMEM = 60 << 20
NEAR = 4
NX = 4


def sigmoid(x):
    return pl.reciprocal(1.0 + jnp.exp(-x), approx=False)


def nn(a, b):
    return jnp.dot(a, b, preferred_element_type=F32)


def nt(a, b):
    return lax.dot_general(a, b, (((1,), (1,)), ((), ())), preferred_element_type=F32)


def tn(a, b):
    return lax.dot_general(a, b, (((0,), (0,)), ((), ())), preferred_element_type=F32)


def scale_of(wide):
    return lax.rsqrt(jnp.mean(wide * wide, -1, keepdims=True) + 1e-6)


def normed(h):
    wide = h.astype(F32)
    return (wide * scale_of(wide)).astype(BF)


def forward_kernel(rows_, h_ref, wg_ref, wu_ref, wd_ref, out_ref, a_ref, next_ref, gate_ref, up_ref, acc_ref):
    step = pl.program_id(0)

    @pl.when(step == 0)
    def _():
        a_ref[...] = normed(h_ref[...])
        acc_ref[...] = jnp.zeros_like(acc_ref)

    for r in range(h_ref.shape[0] // rows_):
        rows = pl.ds(r * rows_, rows_)
        a = a_ref[rows]
        gate = nn(a, wg_ref[...])
        up = nn(a, wu_ref[...])
        gate_ref[rows] = gate
        up_ref[rows] = up
        p = (gate * sigmoid(gate) * up).astype(BF)
        acc_ref[rows] += nn(p, wd_ref[...])

    @pl.when(step == pl.num_programs(0) - 1)
    def _():
        h = h_ref[...] + acc_ref[...].astype(BF)
        out_ref[...] = h
        next_ref[...] = normed(h)


def forward(h, wg, wu, wd, layer, chunk=512, rows=512):
    t, d = h.shape
    ff = wg.shape[2]
    full = pl.BlockSpec((t, d), lambda j: (0, 0))
    wide = pl.BlockSpec((None, d, chunk), lambda j: (layer, 0, j))
    cols = pl.BlockSpec((None, t, chunk), lambda j: (j, 0, 0))
    return pl.pallas_call(
        functools.partial(forward_kernel, rows),
        grid=(ff // chunk,),
        in_specs=[full, wide, wide, pl.BlockSpec((None, chunk, d), lambda j: (layer, j, 0))],
        out_specs=[full] * 3 + [cols] * 2,
        out_shape=[jax.ShapeDtypeStruct((t, d), BF)] * 3 + [jax.ShapeDtypeStruct((ff // chunk, t, chunk), F32)] * 2,
        scratch_shapes=[pltpu.VMEM((t, d), F32)],
        compiler_params=pltpu.CompilerParams(vmem_limit_bytes=VMEM),
        cost_estimate=pl.CostEstimate(flops=6 * t * d * ff, bytes_accessed=8 * t * ff, transcendentals=0),
        name="forward",
    )(h, wg, wu, wd)


def middle(gate, up, dp, rows, p_s, dg_s, du_s):
    dp = dp.astype(BF).astype(F32)
    s = sigmoid(gate)
    silu = gate * s
    p_s[rows] = (silu * up).astype(BF)
    du_s[rows] = (dp * silu).astype(BF)
    dg_s[rows] = (dp * up * (s + silu * (1.0 - s))).astype(BF)


def both_kernel(near, nx, a1, h1, dy, a0, wg, wu, wd, gate0, up0, *refs):
    per = wd.shape[1] // 2 // CHUNK
    far = per - near
    n = near + per
    refs = list(refs)
    take = lambda k: [refs.pop(0) for _ in range(k)]
    stacked, came, *sums = take(2 + n - nx)
    sums = [stacked.at[k] for k in range(nx)] + sums
    (landed,) = take(1)
    saved = take(3)
    (peer_a,) = take(1)
    a_v, dy_v, b_v, da_v, p_s, dg_s, du_s, wg_v, wu_v, wd_v, gate_v, up_v, add_v, grad_v = take(14)
    in_sem, w_sem, g_sem, add_sem, out_sem, save_sem, d_send, d_recv, x_send, x_recv, a_send, a_recv = take(12)
    t_save, t_low, steps = 2 * near, 2 * per, 4 * per
    j = pl.program_id(0)
    rep, dp = lax.axis_index("rep"), lax.axis_index("dp")
    core = lax.rem(dp, 2)
    beside = (rep, dp + 1 - 2 * core)
    across = (rep, lax.rem(dp + 2, 4))
    t = a_v.shape[0]

    def saving(j):
        return (j >= t_save) & (j < t_low)

    def what(j):
        low = j >= t_low
        m = jnp.where(low, per, near)
        k = jnp.where(low, j - t_low, j)
        own = ((k >= 2) & (lax.rem(k, 2) == 0)) | (k == 2 * m - 1)
        number = jnp.where(own, jnp.where(k == 2 * m - 1, m - 1, k // 2 - 1), (k + 1) // 2)
        return own & jnp.logical_not(saving(j)), number, jnp.where(low, near, 0) + number

    def gives(j, own):
        mine = what(j)[0]
        return (j < steps) & jnp.logical_not(saving(j)) & (mine if own else jnp.logical_not(mine))

    def block_of(j):
        own, number, _ = what(j)
        side = jnp.where(own, core, 1 - core)
        k = j - t_save
        near_block = side * per + number
        return jnp.where(saving(j), (k // far) * per + near + lax.rem(k, far), near_block) if far else near_block

    def loads(j, top):
        s = lax.rem(j, 2)
        block = block_of(j)
        cols = pl.ds(pl.multiple_of(block * CHUNK, CHUNK), CHUNK)
        if top:
            return [
                pltpu.make_async_copy(wg.at[1, :, cols], wg_v.at[s], w_sem.at[s, 0]),
                pltpu.make_async_copy(wu.at[1, :, cols], wu_v.at[s], w_sem.at[s, 1]),
                pltpu.make_async_copy(wd.at[1, cols], wd_v.at[s], w_sem.at[s, 2]),
            ]
        return [
            pltpu.make_async_copy(gate0.at[block], gate_v.at[s], g_sem.at[s, 0]),
            pltpu.make_async_copy(up0.at[block], up_v.at[s], g_sem.at[s, 1]),
            pltpu.make_async_copy(wd.at[0, cols], wd_v.at[s], w_sem.at[s, 2]),
        ]

    def load(j, do):
        @pl.when(j < t_low)
        def _():
            for c in loads(j, True):
                do(c)

        @pl.when((j >= t_low) & (j < steps))
        def _():
            for c in loads(j, False):
                do(c)

    start, wait = (lambda c: c.start()), (lambda c: c.wait())
    slot = lax.rem(j, 2)

    def d2d(q, s):
        return pltpu.make_async_remote_copy(
            src_ref=grad_v.at[s], dst_ref=landed.at[q], send_sem=d_send.at[q], recv_sem=d_recv.at[q], device_id=beside, device_id_type=MESH
        )

    def exchange(k):
        return pltpu.make_async_remote_copy(
            src_ref=sums[k], dst_ref=came.at[k], send_sem=x_send.at[k], recv_sem=x_recv.at[k], device_id=across, device_id_type=MESH
        )

    states = pltpu.make_async_remote_copy(
        src_ref=a1, dst_ref=peer_a, send_sem=a_send, recv_sem=a_recv, device_id=across, device_id_type=MESH
    )

    def add_copy(q, s):
        return pltpu.make_async_copy(landed.at[q], add_v.at[s], add_sem.at[s])

    def saves(j, s):
        return [pltpu.make_async_copy(z.at[s], out.at[j - t_save], save_sem.at[s, i]) for i, (z, out) in enumerate(zip((dg_s, du_s, p_s), saved))]

    def late(j):
        low = j >= t_low
        k = jnp.where(low, j - t_low, j)
        return (k == 2) | (k == jnp.where(low, t_low, t_save) - 1)

    def keep(j, do, k_max):
        q = what(j)[2]
        s = lax.rem(j, 2)
        for k in range(k_max):
            pl.when(gives(j, True) & (q == k))(lambda k=k: do(k, s))

    def kept(k, s):
        return pltpu.make_async_copy(grad_v.at[s], sums[k], out_sem.at[s])

    def ship(j):
        pl.when(gives(j, False))(lambda: d2d(what(j)[2], lax.rem(j, 2)).start())
        keep(j, lambda k, s: kept(k, s).start(), n)
        if far:

            @pl.when(saving(j))
            def _():
                for c in saves(j, lax.rem(j, 2)):
                    c.start()

    def settle(j):
        pl.when(gives(j, False))(lambda: d2d(what(j)[2], lax.rem(j, 2)).wait_send())

        def done(k, s):
            kept(k, s).wait()
            if k < nx:
                exchange(k).start()

        keep(j, done, n)
        if far:

            @pl.when(saving(j))
            def _():
                for c in saves(j, lax.rem(j, 2)):
                    c.wait()

    first_loads = [(a1, a_v), (dy, dy_v), (h1, b_v)]

    @pl.when(j == 0)
    def _():
        load(j, start)
        for k, (src, dst) in enumerate(first_loads):
            pltpu.make_async_copy(src, dst, in_sem.at[k]).start()
        barrier = pltpu.get_barrier_semaphore()
        for device in (beside, across):
            pl.semaphore_signal(barrier, inc=1, device_id=device, device_id_type=MESH)
        pl.semaphore_wait(barrier, 2)
        states.start()
        for k, (src, dst) in enumerate(first_loads):
            pltpu.make_async_copy(src, dst, in_sem.at[k]).wait()

    pl.when(j >= 2)(lambda: settle(j - 2))
    pl.when(j >= 1)(lambda: ship(j - 1))
    load(j, wait)
    load(j + 1, start)

    def fetch(j):
        q = what(j)[2]
        d2d(q, lax.rem(j, 2)).wait_recv()
        add_copy(q, lax.rem(j, 2)).start()

    pl.when(gives(j, True) & late(j))(lambda: fetch(j))
    pl.when(gives(j, True))(lambda: add_copy(what(j)[2], slot).wait())
    pl.when(gives(j + 1, True) & jnp.logical_not(late(j + 1)))(lambda: fetch(j + 1))

    @pl.when(gives(j, False))
    def _():
        add_v[slot] = jnp.zeros(add_v.shape[1:], BF)

    p_j, dg_j, du_j = p_s.at[slot], dg_s.at[slot], du_s.at[slot]

    def gradients():
        for k, (left, right) in enumerate(((a_v, dg_j), (a_v, du_j), (dy_v, p_j))):
            grad_v[slot, k] = (tn(left[...], right[...]) + add_v[slot, k].astype(F32)).astype(BF)

    def upper(grads):
        wgj, wuj, wdj = wg_v.at[slot], wu_v.at[slot], wd_v.at[slot]
        for r in range(t // ROWS):
            rows = pl.ds(r * ROWS, ROWS)
            a = a_v[rows]
            middle(nn(a, wgj[...]), nn(a, wuj[...]), nt(dy_v[rows], wdj[...]), rows, p_j, dg_j, du_j)
        if grads:
            gradients()
        for r in range(t // ROWS):
            rows = pl.ds(r * ROWS, ROWS)
            da_v[rows] = jnp.where(j == 0, 0.0, da_v[rows]) + (nt(dg_j[rows], wgj[...]) + nt(du_j[rows], wuj[...]))

    pl.when(j < t_save)(lambda: upper(True))
    if far:
        pl.when(saving(j))(lambda: upper(False))

    @pl.when(j == t_low - 1)
    def _():
        def turn(r, _):
            rows = pl.ds(pl.multiple_of(r * 256, 256), 256)
            wide = b_v[rows].astype(F32)
            da = da_v[rows].astype(BF).astype(F32)
            scale = scale_of(wide)
            dot = jnp.sum(da * wide, -1, keepdims=True)
            dwide = da * scale - wide * (scale * scale * scale * dot * (1.0 / wide.shape[-1]))
            dy_v[rows] = dy_v[rows] + dwide.astype(BF)
            return 0

        lax.fori_loop(0, t // 256, turn, 0)
        c = pltpu.make_async_copy(a0, a_v, in_sem.at[0])
        c.start()
        c.wait()

    @pl.when(j >= t_low)
    def _():
        gj, uj, wdj = gate_v.at[slot], up_v.at[slot], wd_v.at[slot]
        for r in range(t // ROWS):
            rows = pl.ds(r * ROWS, ROWS)
            middle(gj[rows], uj[rows], nt(dy_v[rows], wdj[...]), rows, p_j, dg_j, du_j)
        gradients()

    @pl.when(j == steps - 1)
    def _():
        ship(j)
        settle(j - 1)
        settle(j)
        for k in range(nx):
            exchange(k).wait()
        states.wait()


def both(a1, h1, dy, a0, weights, saved, near, nx):
    t, d = a1.shape
    ff = weights[2].shape[1]
    per = ff // 2 // CHUNK
    n = near + per
    anywhere = pl.BlockSpec(memory_space=pl.ANY)
    chunk = jax.ShapeDtypeStruct((3, d, CHUNK), BF)
    kept = jax.ShapeDtypeStruct((2 * (per - near), t, CHUNK), BF)
    stack = jax.ShapeDtypeStruct((nx, 3, d, CHUNK), BF)
    outs = [stack] * 2 + [chunk] * (n - nx) + [jax.ShapeDtypeStruct((n, 3, d, CHUNK), BF)] + [kept] * 3 + [jax.ShapeDtypeStruct((t, d), BF)]
    dma = pltpu.SemaphoreType.DMA
    out = pl.pallas_call(
        functools.partial(both_kernel, near, nx),
        grid=(4 * per,),
        in_specs=[anywhere] * 9,
        out_specs=[anywhere] * len(outs),
        out_shape=outs,
        scratch_shapes=[pltpu.VMEM((t, d), BF)] * 3
        + [pltpu.VMEM((t, d), F32)]
        + [pltpu.VMEM((2, t, CHUNK), BF)] * 3
        + [pltpu.VMEM((2, d, CHUNK), BF)] * 2
        + [pltpu.VMEM((2, CHUNK, d), BF)]
        + [pltpu.VMEM((2, t, CHUNK), F32)] * 2
        + [pltpu.VMEM((2, 3, d, CHUNK), BF)] * 2
        + [dma((3,)), dma((2, 3)), dma((2, 2)), dma((2,)), dma((2,)), dma((2, 3))]
        + [dma((n,))] * 2
        + [dma((nx,))] * 2
        + [dma, dma],
        compiler_params=pltpu.CompilerParams(vmem_limit_bytes=67_000_000, collective_id=1, has_side_effects=True),
        cost_estimate=pl.CostEstimate(flops=24 * t * d * ff, bytes_accessed=8 * t * ff, transcendentals=0),
        name="backward",
    )(a1, h1, dy, a0, *weights, *saved)
    return out[:2], [[z, None] for z in out[2 : 2 + n - nx]], out[3 + n - nx : 6 + n - nx], out[6 + n - nx]


def adamw_block(gs, w, m, v, new_w, new_m, new_v, sum_ref):
    for i in range(3):
        g = gs[0][i].astype(F32)
        if sum_ref is not None:
            total = (g + gs[1][i].astype(F32)).astype(BF)
            sum_ref[i] = total
            g = total.astype(F32)
        if i == 2:
            g = g.T
        mi = 0.9 * m[i][...] + 0.1 * g
        vi = 0.95 * v[i][...] + 0.05 * g * g
        wi = w[i][...].astype(F32)
        step = mi * lax.rsqrt(vi + 1e-8) + 0.1 * wi
        new_w[i][...] = (wi - 0.02 * step).astype(BF)
        new_m[i][...] = mi
        new_v[i][...] = vi


def shared_kernel(own, aliased, table_ref, a_own, a_peer, dy_own, dy_peer, dg, du, p, wg_ref, wu_ref, wd_ref, *refs):
    refs = list(refs)
    take = lambda k: [refs.pop(0) for _ in range(k)]
    add_ref = take(1)[0] if own else None
    gs = take(1 if own else 2)
    w, m, v = take(3), take(3), take(3)
    take(9 * aliased)
    (out_ref,) = take(1)
    new = take(3), take(3), take(3)
    sum_ref = None if own else take(1)[0]
    a_st, dy_st, dg_s, du_s, p_s, in_sem, save_sem = take(7)
    j, part = pl.program_id(0), pl.program_id(1)
    t = a_own.shape[0]
    width = wd_ref.shape[0]
    per = CHUNK // width
    here = table_ref[0, 0]
    mine = pl.multiple_of(here * t, t)
    theirs = pl.multiple_of((1 - here) * t, t)

    def saves():
        block = table_ref[2, j]
        cols = pl.ds(pl.multiple_of(lax.rem(block, per) * width, width), width)
        return [
            pltpu.make_async_copy(src.at[block // per, :, cols], dst.at[pl.ds(mine, t)], save_sem.at[i])
            for i, (src, dst) in enumerate(((dg, dg_s), (du, du_s), (p, p_s)))
        ]

    @pl.when((j == 0) & (part == 0))
    def _():
        copies = [
            pltpu.make_async_copy(src, dst.at[pl.ds(at, t)], in_sem.at[i])
            for i, (src, dst, at) in enumerate(((a_peer, a_st, theirs), (dy_peer, dy_st, theirs), (a_own, a_st, mine), (dy_own, dy_st, mine)))
        ]
        for c in copies:
            c.start()
        for c in copies:
            c.wait()

    @pl.when(part == 0)
    def _():
        for c in saves():
            c.start()
        for r in range(t // ROWS):
            rows = pl.ds(pl.multiple_of(theirs + r * ROWS, ROWS), ROWS)
            a = a_st[rows]
            middle(nn(a, wg_ref[...]), nn(a, wu_ref[...]), nt(dy_st[rows], wd_ref[...]), rows, p_s, dg_s, du_s)
        adamw_block(gs, w, m, v, *new, sum_ref)

    @pl.when(part == 1)
    def _():
        for c in saves():
            c.wait()
        for k, (left, right) in enumerate(((a_st, dg_s), (a_st, du_s), (dy_st, p_s))):
            g = tn(left[...], right[...])
            if own:
                g += add_ref[k].astype(F32)
            out_ref[k] = g.astype(BF)
        adamw_block(gs, w, m, v, *new, sum_ref)


def shared(table, a_own, a_peer, dy_own, dy_peer, saved, weights, add, gs, moments, new, steps, jobs):
    t, d = a_own.shape
    own = add is not None
    width = ADAM_COLS
    anywhere = pl.BlockSpec(memory_space=pl.ANY)
    wide = pl.BlockSpec((None, d, width), lambda j, p, c: (1, 0, c[1, j]))
    part = pl.BlockSpec((3, d, width), lambda j, p, c: (0, 0, j))

    def job(j, p):
        return jnp.minimum(2 * j + p, jobs - 1)

    stack = pl.BlockSpec((None, 3, d, width), lambda j, p, c: (c[5, job(j, p)], 0, 0, c[6, job(j, p)]))
    across = pl.BlockSpec((None, d, width), lambda j, p, c: (c[3, job(j, p)], 0, c[4, job(j, p)]))
    down = pl.BlockSpec((None, width, d), lambda j, p, c: (c[3, job(j, p)], c[4, job(j, p)], 0))
    kinds = [across, across, down] * 3
    arrays = (*weights, *moments)
    out = [jax.ShapeDtypeStruct((3, d, steps * width), BF)] + [jax.ShapeDtypeStruct(x.shape, x.dtype) for x in arrays]
    dma = pltpu.SemaphoreType.DMA
    before = 11 + own + len(gs) + 9
    out = pl.pallas_call(
        functools.partial(shared_kernel, own, new is not None),
        grid_spec=pltpu.PrefetchScalarGridSpec(
            num_scalar_prefetch=1,
            grid=(steps, 2),
            in_specs=[anywhere] * 7
            + [wide, wide, pl.BlockSpec((None, width, d), lambda j, p, c: (1, c[1, j], 0))]
            + [part] * own
            + [stack] * len(gs)
            + kinds
            + [anywhere] * (9 if new is not None else 0),
            out_specs=[part] + kinds + [stack] * (not own),
            scratch_shapes=[pltpu.VMEM((2 * t, d), BF)] * 2 + [pltpu.VMEM((2 * t, width), BF)] * 3 + [dma((4,)), dma((3,))],
        ),
        out_shape=out + [jax.ShapeDtypeStruct(gs[0].shape, BF)] * (not own),
        input_output_aliases={before + i: 1 + i for i in range(9)} if new is not None else {},
        compiler_params=pltpu.CompilerParams(vmem_limit_bytes=67_000_000),
        cost_estimate=pl.CostEstimate(flops=18 * t * d * width * steps, bytes_accessed=22 * 3 * d * width * jobs, transcendentals=0),
        name="shared_own" if own else "shared_other",
    )(table, a_own, a_peer, dy_own, dy_peer, *saved, *weights, *([add] if own else []), *gs, *arrays, *(new or ()))
    return out[0], out[1:10], out[10:]


def adamw_kernel(own, aliased, chunks, off_ref, *refs):
    gs, refs = refs[: (1 + own) * chunks], refs[(1 + own) * chunks :]
    w, m, v = refs[0:3], refs[3:6], refs[6:9]
    refs = refs[9 + 9 * aliased :]
    new_w, new_m, new_v = refs[0:3], refs[3:6], refs[6:9]

    def work(g_refs):
        adamw_block(g_refs, w, m, v, new_w, new_m, new_v, refs[9] if own else None)

    per = CHUNK // ADAM_COLS
    for k in range(chunks if own else 1):
        g_refs = gs[k * (1 + own) : (k + 1) * (1 + own)]
        if own and chunks > 1:
            pl.when(pl.program_id(0) // per == k)(functools.partial(work, g_refs))
        else:
            work(g_refs)


def adamw(off, gs, weights, m, v, new, layer, own):
    d = weights[0].shape[1]
    chunks = len(gs) // 2 if own else 1
    unit = chunks * gs[0].shape[2]
    per = CHUNK // ADAM_COLS
    wide = pl.BlockSpec((None, d, ADAM_COLS), lambda j, o: (layer, 0, o[0] + j))
    tall = pl.BlockSpec((None, ADAM_COLS, d), lambda j, o: (layer, o[0] + j, 0))
    grad = pl.BlockSpec((3, d, ADAM_COLS), lambda j, o: (0, 0, j))

    def part(k):
        return pl.BlockSpec((3, d, ADAM_COLS), lambda j, o: (0, 0, jnp.clip(j - k * per, 0, per - 1)))

    kinds = [wide, wide, tall] * 3
    shapes = [jax.ShapeDtypeStruct(x.shape, x.dtype) for x in (*weights, *m, *v)]
    out = pl.pallas_call(
        functools.partial(adamw_kernel, own, new is not None, chunks),
        grid_spec=pltpu.PrefetchScalarGridSpec(
            num_scalar_prefetch=1,
            grid=(unit // ADAM_COLS,),
            in_specs=([part(k // 2) for k in range(2 * chunks)] if own else [grad])
            + kinds
            + ([pl.BlockSpec(memory_space=pl.ANY)] * 9 if new is not None else []),
            out_specs=kinds + [grad] * own,
        ),
        out_shape=shapes + [jax.ShapeDtypeStruct((3, d, unit), BF)] * own,
        input_output_aliases={10 + len(gs) + i: i for i in range(9)} if new is not None else {},
        compiler_params=pltpu.CompilerParams(vmem_limit_bytes=VMEM),
        cost_estimate=pl.CostEstimate(flops=int(8 * 3 * d * unit * 30), bytes_accessed=22 * 3 * d * unit, transcendentals=0),
        name="adamw_own" if own else "adamw_other",
    )(off, *gs, *weights, *m, *v, *(new or ()))
    return out[:9], out[9:]


ORDER = (
    "p0", "F", "G", "x4", "x5", "Y0", "s0", "t0", "x6", "x7", "Z0", "k0",
    "x8", "A4+5", "h4", "x9", "C0", "B4+5", "D0", "A6", "h6", "A7", "h7", "B6",
    "B7", "A8", "h8", "A9", "h9", "B8", "B9",
)


def chunks_of(name):
    first, *more = name[1:].split("+")
    return range(int(first), 1 + int(more[0] if more else first))


def solution(mesh):
    reps, dps = mesh.shape["rep"], mesh.shape["dp"]

    def pairs(to):
        return [(r * dps + i, r * dps + to(i)) for r in range(reps) for i in range(dps)]

    across = pairs(lambda i: (i + 2) % dps)
    beside = pairs(lambda i: i ^ 1)

    def step(x, dy, *arrays):
        weights, m, v = (arrays[i : i + 3] for i in (0, 3, 6))
        core = lax.axis_index("dp") % 2
        half = weights[0].shape[2] // 2
        per = half // CHUNK
        have = {}
        new = None

        def offset(side, number):
            return ((side * half + number * CHUNK) // ADAM_COLS).astype(jnp.int32).reshape(1)

        def send(z, to):
            return lax.ppermute(z, AXES, to)

        def table(side):
            far, parts = per - NEAR, CHUNK // ADAM_COLS
            k = jnp.arange(far * parts, dtype=jnp.int32)
            i = jnp.arange(NX * parts, dtype=jnp.int32)
            chunk, layer = i // parts, (i // parts < NEAR).astype(jnp.int32)
            number = chunk - (1 - layer) * NEAR
            rows = [where, (side * per + NEAR) * parts + k, side * far * parts + k, layer, (side * per + number) * parts + i % parts, chunk, i % parts]
            width = max(far, NX) * parts
            return jnp.stack([jnp.pad(r.astype(jnp.int32), (0, width - r.shape[0])) for r in rows])

        where = (lax.axis_index("dp") // 2).astype(jnp.int32).reshape(1)
        moments = (*m, *v)
        steps, jobs = (per - NEAR) * (CHUNK // ADAM_COLS), NX * (CHUNK // ADAM_COLS)
        for name in ORDER:
            kind = name[0]
            if kind == "p":
                peer_dy = send(dy[0], across)
            elif kind == "F":
                h1, a0, a1, gate0, up0 = forward(x[0], *weights, 0)
            elif kind == "G":
                stacks, pair, saved, peer_a = both(a1, h1, dy[0], a0, weights, (gate0, up0), NEAR, NX)
            elif kind == "Y":
                sides = jnp.concatenate([table(1 - core)[:3], table(core)[3:]])
                far, new, (total,) = shared(
                    sides, a1, peer_a, dy[0], peer_dy, saved, weights, None, stacks, moments, new, steps, jobs
                )
            elif kind == "s":
                far = send(far, beside)
            elif kind == "t":
                total = send(total, beside)
            elif kind == "Z":
                both_sides = jnp.concatenate([table(core)[:3], table(1 - core)[3:]])
                far, new, _ = shared(both_sides, a1, peer_a, dy[0], peer_dy, saved, weights, far, [total], moments, new, steps, jobs)
            elif kind == "k":
                far_other = send(far, beside)
            elif kind in "CD":
                side, g = (core, far) if kind == "C" else (1 - core, far_other)
                new, _ = adamw(offset(side, NEAR), [g], weights, m, v, new, 1, 0)
            elif kind == "x":
                k = int(name[1:]) - NX
                pair[k][1] = send(pair[k][0], across)
            elif kind == "h":
                have[name[1:]] = send(have["A" + name[1:]], beside)
            else:
                ks = chunks_of(name)
                number, first = ks[0] - NEAR, str(ks[0])
                if kind == "A":
                    gs = [z for k in ks for z in pair[k - NX]]
                    new, (have["A" + first],) = adamw(offset(core, number), gs, weights, m, v, new, 0, 1)
                else:
                    new, _ = adamw(offset(1 - core, number), [have[first]], weights, m, v, new, 0, 0)
        return tuple(new)

    return jax.shard_map(
        step,
        mesh=mesh,
        in_specs=(P(("rep", "dp"), None, None),) * 2 + (P(None, None, None),) * 9,
        out_specs=(P("rep", None, None),) * 9,
        check_vma=False,
    )
```

time: 906 us -> 827 us (0.913)
  waiting for transfers between devices: 225 us -> 138 us
    pallas_call x1 -> x3, Pallas kernels: 326 us -> 424 us  [the longest x1 285 us: both(): pl.pallas_call(functools.partial(both_kernel, near, nx), grid=(4 * per,),...]
    pallas_call x18 -> x12, Pallas kernels: 262 us -> 170 us  [adamw(): pl.pallas_call(functools.partial(adamw_kernel, own, new is not None, chun...]
    ppermute x16 -> x15, waiting for transfers between devices: 225 us -> 138 us  [send(): return lax.ppermute(z, AXES, to)]
  transfers between devices with their start and end apart: 16 -> 15, of which waited for: 8 -> 5; matrix products, arithmetic and copies ran while one was open for 0% -> 0% of each run, Pallas kernels for 23% -> 69%
where the time goes in v2:
time: 827 us; the launch traced here: 821 us
  Pallas kernels  670 us (81%)
  waiting for transfers between devices  138 us (17%)
  starting transfers between devices  10.6 us (1%)
    pallas_call x1, Pallas kernels, both(): pl.pallas_call(functools.partial(both_kernel, near, nx), grid=(4 * per,),...  285 us
    pallas_call x12, Pallas kernels, adamw(): pl.pallas_call(functools.partial(adamw_kernel, own, new is not None, chun...  170 us
    pallas_call x2, Pallas kernels, shared(): pl.pallas_call(functools.partial(shared_kernel, own, new is not None), gr...  139 us
    ppermute x15, waiting for transfers between devices, send(): return lax.ppermute(z, AXES, to)  138 us
    pallas_call x1, Pallas kernels, forward(): pl.pallas_call(functools.partial(forward_kernel, rows), grid=(ff // chunk...  75.7 us
  transfers between devices with their start and end apart: 15, of which 5 were waited for; matrix products, arithmetic and copies ran while one was open for 0% of the time, Pallas kernels for 69%

profile of v2, /device:TPU:0, one launch (start us, length us, event | category | flops | bytes accessed | tf_op | source)
XLA Modules:
  0.0 821.2 jit_solution(5218264530779132980)
XLA Ops:
  0.6 3.3 collective-permute-start.4
  4.0 75.7 %forward.1 = (bf16[2048,768]{1,0:T(8,128)(2,1)}, bf16[2048,768]{1,0:T(8,128)(2,1)}, bf16[2048,768]{1,0:T(8,128)(2,1)}, f32[12,2048,512]{2,1,0:T(8,128)}, f32[12,2048,512]{2,1,0:T(8,128)}) custom-call(bf16[2048,768]{1,0:T(8,128)(2,1)} %bitcast.27, bf16[2,768,6144]{2,1,0:T(8,128)(2,1)} %refs_1_.13, bf16[2,768,6144]{2,1,0:T(8,128)(2,1)} %refs_2_.25, ...), custom_call_target="tpu_custom_call" | custom-call | flops 57982058496 | bytes 100663296 | tf_op jit(solution)/shard_map/forward/pallas_call | solution.py:78
  79.7 285.3 %backward.1 = (bf16[4,3,768,512]{3,2,1,0:T(8,128)(2,1)}, bf16[4,3,768,512]{3,2,1,0:T(8,128)(2,1)}, bf16[3,768,512]{2,1,0:T(8,128)(2,1)}, bf16[3,768,512]{2,1,0:T...) custom-call(bf16[2048,768]{1,0:T(8,128)(2,1)} %get-tuple-element.151, ...), custom_call_target="tpu_custom_call" | custom-call | flops 231928233984 | bytes 100663296 | tf_op jit(solution)/shard_map/backward/pallas_call | solution.py:334
  365.1 0.6 concatenate.7.table_ref
  365.7 0.0 collective-permute-done.4.dy_peer
  365.7 72.4 %shared_other.1 = (bf16[3,768,1024]{2,1,0:T(8,128)(2,1)}, bf16[2,768,6144]{2,1,0:T(8,128)(2,1)}, bf16[2,768,6144]{2,1,0:T(8,128)(2,1)}, bf16[2,6144,768]{2,1,0:T...) custom-call(s32[7,8]{1,0:T(8,128)} %concatenate.7.table_ref, ...), custom_call_target="tpu_custom_call" | custom-call | flops 28991029248 | bytes 103809024 | tf_op jit(solution)/shard_map/shared_other/pallas_call | solution.py:455
  438.1 0.0 collective-permute-start.6
  438.1 0.5 collective-permute-start.5
  438.6 0.0 collective-permute-start.8
  438.7 2.0 collective-permute-start.9
  440.7 0.6 concatenate.6.table_ref
  441.3 18.5 %collective-permute-done.5.refs_0_ = bf16[3,768,1024]{2,1,0:T(8,128)(2,1)} collective-permute-done((bf16[3,768,1024]{2,1,0:T(8,128)(2,1)}, bf16[3,768,1024]{2,1,0:T(8,128)(2,1)}, u32[]{:S(2)}, u32[]{:S(2)}) %collective-permute-start.5) | collective-permute-done | bytes 4718624 | tf_op jit(solution)/shard_map/ppermute | solution.py:562
  459.9 0.0 collective-permute-done.6.refs_1_
  459.9 66.8 %shared_own.1 = (bf16[3,768,1024]{2,1,0:T(8,128)(2,1)}, bf16[2,768,6144]{2,1,0:T(8,128)(2,1)}, bf16[2,768,6144]{2,1,0:T(8,128)(2,1)}, bf16[2,6144,768]{2,1,0:T(8...) custom-call(s32[7,8]{1,0:T(8,128)} %concatenate.6.table_ref, ...), custom_call_target="tpu_custom_call", output_to_operand_aliasing={{1}: (22, {}), {2}: (23, {}), {3}: (24, {}), {4}: (25, {}),... | custom-call | flops 28991029248 | bytes 103809024 | tf_op jit(solution)/shard_map/shared_own/pallas_call | solution.py:455
  526.6 0.0 collective-permute-done.8.refs_1_
  526.7 16.0 %collective-permute-done.9.refs_3_ = bf16[3,768,512]{2,1,0:T(8,128)(2,1)} collective-permute-done((bf16[3,768,512]{2,1,0:T(8,128)(2,1)}, bf16[3,768,512]{2,1,0:T(8,128)(2,1)}, u32[]{:S(2)}, u32[]{:S(2)}) %collective-permute-start.9) | collective-permute-done | bytes 2359328 | tf_op jit(solution)/shard_map/ppermute | solution.py:562
  542.7 24.0 %adamw_own.5 = (bf16[2,768,6144]{2,1,0:T(8,128)(2,1)}, bf16[2,768,6144]{2,1,0:T(8,128)(2,1)}, bf16[2,6144,768]{2,1,0:T(8,128)(2,1)}, f32[2,768,6144]{2,1,0:T(8,1...) custom-call(s32[1]{0:T(128)} %bitcast.16.off_ref, ...), custom_call_target="tpu_custom_call", output_to_operand_aliasing={{0}: (14, {}), {1}: (15, {}), {2}: (16, {}), {3}: (17, {}),... | custom-call | flops 566231040 | bytes 51904512 | tf_op jit(solution)/shard_map/adamw_own/pallas_call | solution.py:510
  566.7 0.0 collective-permute-start.10
  566.7 0.5 collective-permute-start.7
  567.2 0.3 collective-permute-start.3
  567.5 1.7 collective-permute-start.2
  569.3 18.8 %adamw_other.7 = (bf16[2,768,6144]{2,1,0:T(8,128)(2,1)}, bf16[2,768,6144]{2,1,0:T(8,128)(2,1)}, bf16[2,6144,768]{2,1,0:T(8,128)(2,1)}, f32[2,768,6144]{2,1,0:T(8...) custom-call(s32[1]{0:T(128)} %bitcast.4.off_ref, ...), custom_call_target="tpu_custom_call", output_to_operand_aliasing={{0}: (11, {}), {1}: (12, {}), {2}: (13, {}), {3}: (14, {}),... | custom-call | flops 566231040 | bytes 51904512 | tf_op jit(solution)/shard_map/adamw_other/pallas_call | solution.py:510
  588.0 0.0 collective-permute-done.10.refs_0_
  588.1 19.0 %adamw_other.8 = (bf16[2,768,6144]{2,1,0:T(8,128)(2,1)}, bf16[2,768,6144]{2,1,0:T(8,128)(2,1)}, bf16[2,6144,768]{2,1,0:T(8,128)(2,1)}, f32[2,768,6144]{2,1,0:T(8...) custom-call(s32[1]{0:T(128)} %bitcast.15.off_ref, ...), custom_call_target="tpu_custom_call", output_to_operand_aliasing={{0}: (11, {}), {1}: (12, {}), {2}: (13, {}), {3}: (14, {}),... | custom-call | flops 566231040 | bytes 51904512 | tf_op jit(solution)/shard_map/adamw_other/pallas_call | solution.py:510
  607.1 0.0 collective-permute-done.7.refs_0_
  607.1 18.8 %adamw_other.9 = (bf16[2,768,6144]{2,1,0:T(8,128)(2,1)}, bf16[2,768,6144]{2,1,0:T(8,128)(2,1)}, bf16[2,6144,768]{2,1,0:T(8,128)(2,1)}, f32[2,768,6144]{2,1,0:T(8...) custom-call(s32[1]{0:T(128)} %bitcast.8.off_ref, ...), custom_call_target="tpu_custom_call", output_to_operand_aliasing={{0}: (11, {}), {1}: (12, {}), {2}: (13, {}), {3}: (14, {}),... | custom-call | flops 566231040 | bytes 51904512 | tf_op jit(solution)/shard_map/adamw_other/pallas_call | solution.py:510
  625.9 0.0 collective-permute-done.3.refs_1_
  625.9 11.9 %adamw_own.6 = (bf16[2,768,6144]{2,1,0:T(8,128)(2,1)}, bf16[2,768,6144]{2,1,0:T(8,128)(2,1)}, bf16[2,6144,768]{2,1,0:T(8,128)(2,1)}, f32[2,768,6144]{2,1,0:T(8,1...) custom-call(s32[1]{0:T(128)} %bitcast.7.off_ref, ...), custom_call_target="tpu_custom_call", output_to_operand_aliasing={{0}: (12, {}), {1}: (13, {}), {2}: (14, {}), {3}: (15, {}),... | custom-call | flops 283115520 | bytes 25952256 | tf_op jit(solution)/shard_map/adamw_own/pallas_call | solution.py:510
  637.8 0.0 collective-permute-start.12
  637.9 33.4 %collective-permute-done.2.refs_1_ = bf16[3,768,512]{2,1,0:T(8,128)(2,1)} collective-permute-done((bf16[3,768,512]{2,1,0:T(8,128)(2,1)}, bf16[3,768,512]{2,1,0:T(8,128)(2,1)}, u32[]{:S(2)}, u32[]{:S(2)}) %collective-permute-start.2) | collective-permute-done | bytes 2359328 | tf_op jit(solution)/shard_map/ppermute | solution.py:562
  671.3 12.0 %adamw_own.7 = (bf16[2,768,6144]{2,1,0:T(8,128)(2,1)}, bf16[2,768,6144]{2,1,0:T(8,128)(2,1)}, bf16[2,6144,768]{2,1,0:T(8,128)(2,1)}, f32[2,768,6144]{2,1,0:T(8,1...) custom-call(s32[1]{0:T(128)} %bitcast.6.off_ref, ...), custom_call_target="tpu_custom_call", output_to_operand_aliasing={{0}: (12, {}), {1}: (13, {}), {2}: (14, {}), {3}: (15, {}),... | custom-call | flops 283115520 | bytes 25952256 | tf_op jit(solution)/shard_map/adamw_own/pallas_call | solution.py:510
  683.3 0.0 collective-permute-start.11
  683.4 0.3 collective-permute-start.1
  683.7 1.7 collective-permute-start
  685.4 0.0 collective-permute-done.12.refs_0_
  685.4 10.3 %adamw_other.10 = (bf16[2,768,6144]{2,1,0:T(8,128)(2,1)}, bf16[2,768,6144]{2,1,0:T(8,128)(2,1)}, bf16[2,6144,768]{2,1,0:T(8,128)(2,1)}, f32[2,768,6144]{2,1,0:T(...) custom-call(s32[1]{0:T(128)} %bitcast.17.off_ref, ...), custom_call_target="tpu_custom_call", output_to_operand_aliasing={{0}: (11, {}), {1}: (12, {}), {2}: (13, {}), {3}: (14, {}),... | custom-call | flops 283115520 | bytes 25952256 | tf_op jit(solution)/shard_map/adamw_other/pallas_call | solution.py:510
  695.7 0.0 collective-permute-done.11.refs_0_
  695.7 10.3 %adamw_other.11 = (bf16[2,768,6144]{2,1,0:T(8,128)(2,1)}, bf16[2,768,6144]{2,1,0:T(8,128)(2,1)}, bf16[2,6144,768]{2,1,0:T(8,128)(2,1)}, f32[2,768,6144]{2,1,0:T(...) custom-call(s32[1]{0:T(128)} %bitcast.5.off_ref, ...), custom_call_target="tpu_custom_call", output_to_operand_aliasing={{0}: (11, {}), {1}: (12, {}), {2}: (13, {}), {3}: (14, {}),... | custom-call | flops 283115520 | bytes 25952256 | tf_op jit(solution)/shard_map/adamw_other/pallas_call | solution.py:510
  706.0 31.8 %collective-permute-done.1.refs_1_ = bf16[3,768,512]{2,1,0:T(8,128)(2,1)} collective-permute-done((bf16[3,768,512]{2,1,0:T(8,128)(2,1)}, bf16[3,768,512]{2,1,0:T(8,128)(2,1)}, u32[]{:S(2)}, u32[]{:S(2)}) %collective-permute-start.1) | collective-permute-done | bytes 2359328 | tf_op jit(solution)/shard_map/ppermute | solution.py:562
  737.8 12.1 %adamw_own.8 = (bf16[2,768,6144]{2,1,0:T(8,128)(2,1)}, bf16[2,768,6144]{2,1,0:T(8,128)(2,1)}, bf16[2,6144,768]{2,1,0:T(8,128)(2,1)}, f32[2,768,6144]{2,1,0:T(8,1...) custom-call(s32[1]{0:T(128)} %bitcast.4.off_ref, ...), custom_call_target="tpu_custom_call", output_to_operand_aliasing={{0}: (12, {}), {1}: (13, {}), {2}: (14, {}), {3}: (15, {}),... | custom-call | flops 283115520 | bytes 25952256 | tf_op jit(solution)/shard_map/adamw_own/pallas_call | solution.py:510
  749.9 0.0 collective-permute-start.14
  750.0 37.9 %collective-permute-done.refs_1_ = bf16[3,768,512]{2,1,0:T(8,128)(2,1)} collective-permute-done((bf16[3,768,512]{2,1,0:T(8,128)(2,1)}, bf16[3,768,512]{2,1,0:T(8,128)(2,1)}, u32[]{:S(2)}, u32[]{:S(2)}) %collective-permute-start) | collective-permute-done | bytes 2359328 | tf_op jit(solution)/shard_map/ppermute | solution.py:562
  787.9 11.8 %adamw_own.9 = (bf16[2,768,6144]{2,1,0:T(8,128)(2,1)}, bf16[2,768,6144]{2,1,0:T(8,128)(2,1)}, bf16[2,6144,768]{2,1,0:T(8,128)(2,1)}, f32[2,768,6144]{2,1,0:T(8,1...) custom-call(s32[1]{0:T(128)} %bitcast.1.off_ref, ...), custom_call_target="tpu_custom_call", output_to_operand_aliasing={{0}: (12, {}), {1}: (13, {}), {2}: (14, {}), {3}: (15, {}),... | custom-call | flops 283115520 | bytes 25952256 | tf_op jit(solution)/shard_map/adamw_own/pallas_call | solution.py:510
  799.7 0.0 collective-permute-start.13
  799.8 0.0 collective-permute-done.14.refs_0_
  799.8 10.3 %adamw_other.12 = (bf16[2,768,6144]{2,1,0:T(8,128)(2,1)}, bf16[2,768,6144]{2,1,0:T(8,128)(2,1)}, bf16[2,6144,768]{2,1,0:T(8,128)(2,1)}, f32[2,768,6144]{2,1,0:T(...) custom-call(s32[1]{0:T(128)} %bitcast.8.off_ref, ...), custom_call_target="tpu_custom_call", output_to_operand_aliasing={{0}: (11, {}), {1}: (12, {}), {2}: (13, {}), {3}: (14, {}),... | custom-call | flops 283115520 | bytes 25952256 | tf_op jit(solution)/shard_map/adamw_other/pallas_call | solution.py:510
  810.1 0.0 collective-permute-done.13.refs_0_
  810.1 10.6 %adamw_other.13 = (bf16[2,768,6144]{2,1,0:T(8,128)(2,1)}, bf16[2,768,6144]{2,1,0:T(8,128)(2,1)}, bf16[2,6144,768]{2,1,0:T(8,128)(2,1)}, f32[2,768,6144]{2,1,0:T(...) custom-call(s32[1]{0:T(128)} %bitcast.off_ref, ...), custom_call_target="tpu_custom_call", output_to_operand_aliasing={{0}: (11, {}), {1}: (12, {}), {2}: (13, {}), {3}: (14, {}),... | custom-call | flops 283115520 | bytes 25952256 | tf_op jit(solution)/shard_map/adamw_other/pallas_call | solution.py:510
  (11 shorter events, 0.1 us)
Async XLA Ops:
  0.6 365.1 %collective-permute-start.4 = (bf16[2048,768]{1,0:T(8,128)(2,1)}, bf16[2048,768]{1,0:T(8,128)(2,1)}, u32[]{:S(2)}, u32[]{:S(2)}) collective-permute-start(bf16[2048,768]{1,0:T(8,128)(2,1)} %bitcast.23), channel_id=1, source_target_pairs={{0,2},{1,3},{2,0},{3,1},{4,6},{5,7},{6,4},{7,5}} | collective-permute-start | bytes 9437192 | tf_op jit(solution)/shard_map/ppermute | solution.py:562
  438.1 21.8 %collective-permute-start.6 = (bf16[4,3,768,512]{3,2,1,0:T(8,128)(2,1)}, bf16[4,3,768,512]{3,2,1,0:T(8,128)(2,1)}, u32[]{:S(2)}, u32[]{:S(2)}) collective-permute-start(bf16[4,3,768,512]{3,2,1,0:T(8,128)(2,1)} %get-tuple-element.167), channel_id=1, source_target_pairs={{0,1},{1,0},{2,3},{3,2},{4,5},{5,4},{6,7},{7,6}} | collective-permute-start | bytes 28311560 | tf_op jit(solution)/shard_map/ppermute | solution.py:562
  438.1 21.7 %collective-permute-start.5 = (bf16[3,768,1024]{2,1,0:T(8,128)(2,1)}, bf16[3,768,1024]{2,1,0:T(8,128)(2,1)}, u32[]{:S(2)}, u32[]{:S(2)}) collective-permute-start(bf16[3,768,1024]{2,1,0:T(8,128)(2,1)} %get-tuple-element.166), channel_id=1, source_target_pairs={{0,1},{1,0},{2,3},{3,2},{4,5},{5,4},{6,7},{7,6}} | collective-permute-start | bytes 14155784 | tf_op jit(solution)/shard_map/ppermute | solution.py:562
  438.6 88.0 %collective-permute-start.8 = (bf16[3,768,512]{2,1,0:T(8,128)(2,1)}, bf16[3,768,512]{2,1,0:T(8,128)(2,1)}, u32[]{:S(2)}, u32[]{:S(2)}) collective-permute-start(bf16[3,768,512]{2,1,0:T(8,128)(2,1)} %get-tuple-element.178.refs_0_), channel_id=1, source_target_pairs={{0,2},{1,3},{2,0},{3,1},{4,6},{5,7},{6,4},{7,5}} | collective-permute-start | bytes 7077896 | tf_op jit(solution)/shard_map/ppermute | solution.py:562
  438.7 104.0 %collective-permute-start.9 = (bf16[3,768,512]{2,1,0:T(8,128)(2,1)}, bf16[3,768,512]{2,1,0:T(8,128)(2,1)}, u32[]{:S(2)}, u32[]{:S(2)}) collective-permute-start(bf16[3,768,512]{2,1,0:T(8,128)(2,1)} %get-tuple-element.179.refs_2_), channel_id=1, source_target_pairs={{0,2},{1,3},{2,0},{3,1},{4,6},{5,7},{6,4},{7,5}} | collective-permute-start | bytes 7077896 | tf_op jit(solution)/shard_map/ppermute | solution.py:562
  566.7 21.4 %collective-permute-start.10 = (bf16[3,768,1024]{2,1,0:T(8,128)(2,1)}, bf16[3,768,1024]{2,1,0:T(8,128)(2,1)}, u32[]{:S(2)}, u32[]{:S(2)}) collective-permute-start(bf16[3,768,1024]{2,1,0:T(8,128)(2,1)} %get-tuple-element.189), channel_id=1, source_target_pairs={{0,1},{1,0},{2,3},{3,2},{4,5},{5,4},{6,7},{7,6}} | collective-permute-start | bytes 14155784 | tf_op jit(solution)/shard_map/ppermute | solution.py:562
  566.7 40.3 %collective-permute-start.7 = (bf16[3,768,1024]{2,1,0:T(8,128)(2,1)}, bf16[3,768,1024]{2,1,0:T(8,128)(2,1)}, u32[]{:S(2)}, u32[]{:S(2)}) collective-permute-start(bf16[3,768,1024]{2,1,0:T(8,128)(2,1)} %get-tuple-element.177.refs_0_), channel_id=1, source_target_pairs={{0,1},{1,0},{2,3},{3,2},{4,5},{5,4},{6,7},{7,6}} | collective-permute-start | bytes 14155784 | tf_op jit(solution)/shard_map/ppermute | solution.py:562
  567.2 58.7 %collective-permute-start.3 = (bf16[3,768,512]{2,1,0:T(8,128)(2,1)}, bf16[3,768,512]{2,1,0:T(8,128)(2,1)}, u32[]{:S(2)}, u32[]{:S(2)}) collective-permute-start(bf16[3,768,512]{2,1,0:T(8,128)(2,1)} %get-tuple-element.159.refs_0_), channel_id=1, source_target_pairs={{0,2},{1,3},{2,0},{3,1},{4,6},{5,7},{6,4},{7,5}} | collective-permute-start | bytes 7077896 | tf_op jit(solution)/shard_map/ppermute | solution.py:562
  567.5 103.8 %collective-permute-start.2 = (bf16[3,768,512]{2,1,0:T(8,128)(2,1)}, bf16[3,768,512]{2,1,0:T(8,128)(2,1)}, u32[]{:S(2)}, u32[]{:S(2)}) collective-permute-start(bf16[3,768,512]{2,1,0:T(8,128)(2,1)} %get-tuple-element.158.refs_0_), channel_id=1, source_target_pairs={{0,2},{1,3},{2,0},{3,1},{4,6},{5,7},{6,4},{7,5}} | collective-permute-start | bytes 7077896 | tf_op jit(solution)/shard_map/ppermute | solution.py:562
  637.8 47.6 %collective-permute-start.12 = (bf16[3,768,512]{2,1,0:T(8,128)(2,1)}, bf16[3,768,512]{2,1,0:T(8,128)(2,1)}, u32[]{:S(2)}, u32[]{:S(2)}) collective-permute-start(bf16[3,768,512]{2,1,0:T(8,128)(2,1)} %get-tuple-element.236), channel_id=1, source_target_pairs={{0,1},{1,0},{2,3},{3,2},{4,5},{5,4},{6,7},{7,6}} | collective-permute-start | bytes 7077896 | tf_op jit(solution)/shard_map/ppermute | solution.py:562
  683.3 12.4 %collective-permute-start.11 = (bf16[3,768,512]{2,1,0:T(8,128)(2,1)}, bf16[3,768,512]{2,1,0:T(8,128)(2,1)}, u32[]{:S(2)}, u32[]{:S(2)}) collective-permute-start(bf16[3,768,512]{2,1,0:T(8,128)(2,1)} %get-tuple-element.235), channel_id=1, source_target_pairs={{0,1},{1,0},{2,3},{3,2},{4,5},{5,4},{6,7},{7,6}} | collective-permute-start | bytes 7077896 | tf_op jit(solution)/shard_map/ppermute | solution.py:562
  683.4 54.5 %collective-permute-start.1 = (bf16[3,768,512]{2,1,0:T(8,128)(2,1)}, bf16[3,768,512]{2,1,0:T(8,128)(2,1)}, u32[]{:S(2)}, u32[]{:S(2)}) collective-permute-start(bf16[3,768,512]{2,1,0:T(8,128)(2,1)} %get-tuple-element.157.refs_0_), channel_id=1, source_target_pairs={{0,2},{1,3},{2,0},{3,1},{4,6},{5,7},{6,4},{7,5}} | collective-permute-start | bytes 7077896 | tf_op jit(solution)/shard_map/ppermute | solution.py:562
  683.7 104.2 %collective-permute-start = (bf16[3,768,512]{2,1,0:T(8,128)(2,1)}, bf16[3,768,512]{2,1,0:T(8,128)(2,1)}, u32[]{:S(2)}, u32[]{:S(2)}) collective-permute-start(bf16[3,768,512]{2,1,0:T(8,128)(2,1)} %get-tuple-element.156.refs_0_), channel_id=1, source_target_pairs={{0,2},{1,3},{2,0},{3,1},{4,6},{5,7},{6,4},{7,5}} | collective-permute-start | bytes 7077896 | tf_op jit(solution)/shard_map/ppermute | solution.py:562
  749.9 49.9 %collective-permute-start.14 = (bf16[3,768,512]{2,1,0:T(8,128)(2,1)}, bf16[3,768,512]{2,1,0:T(8,128)(2,1)}, u32[]{:S(2)}, u32[]{:S(2)}) collective-permute-start(bf16[3,768,512]{2,1,0:T(8,128)(2,1)} %get-tuple-element.274), channel_id=1, source_target_pairs={{0,1},{1,0},{2,3},{3,2},{4,5},{5,4},{6,7},{7,6}} | collective-permute-start | bytes 7077896 | tf_op jit(solution)/shard_map/ppermute | solution.py:562
  799.7 10.4 %collective-permute-start.13 = (bf16[3,768,512]{2,1,0:T(8,128)(2,1)}, bf16[3,768,512]{2,1,0:T(8,128)(2,1)}, u32[]{:S(2)}, u32[]{:S(2)}) collective-permute-start(bf16[3,768,512]{2,1,0:T(8,128)(2,1)} %get-tuple-element.273), channel_id=1, source_target_pairs={{0,1},{1,0},{2,3},{3,2},{4,5},{5,4},{6,7},{7,6}} | collective-permute-start | bytes 7077896 | tf_op jit(solution)/shard_map/ppermute | solution.py:562

commit v3 on v2

--- a/solution.py
+++ b/solution.py
@@ -14,6 +14,7 @@
 CHUNK = 512
 ROWS = 512
 ADAM_COLS = 256
+ADAM_ROWS = 128
 VMEM = 60 << 20
 NEAR = 4
 NX = 4
@@ -44,7 +45,7 @@
     return (wide * scale_of(wide)).astype(BF)
 
 
-def forward_kernel(rows_, h_ref, wg_ref, wu_ref, wd_ref, out_ref, a_ref, next_ref, gate_ref, up_ref, acc_ref):
+def forward_kernel(rows_, h_ref, wg_ref, wu_ref, wd_ref, out_ref, a_ref, next_ref, gate_ref, up_ref, acc_ref, p_s):
     step = pl.program_id(0)
 
     @pl.when(step == 0)
@@ -59,8 +60,10 @@
         up = nn(a, wu_ref[...])
         gate_ref[rows] = gate
         up_ref[rows] = up
-        p = (gate * sigmoid(gate) * up).astype(BF)
-        acc_ref[rows] += nn(p, wd_ref[...])
+        p_s[rows] = (gate * sigmoid(gate) * up).astype(BF)
+    for r in range(h_ref.shape[0] // rows_):
+        rows = pl.ds(r * rows_, rows_)
+        acc_ref[rows] += nn(p_s[rows], wd_ref[...])
 
     @pl.when(step == pl.num_programs(0) - 1)
     def _():
@@ -81,7 +84,7 @@
         in_specs=[full, wide, wide, pl.BlockSpec((None, chunk, d), lambda j: (layer, j, 0))],
         out_specs=[full] * 3 + [cols] * 2,
         out_shape=[jax.ShapeDtypeStruct((t, d), BF)] * 3 + [jax.ShapeDtypeStruct((ff // chunk, t, chunk), F32)] * 2,
-        scratch_shapes=[pltpu.VMEM((t, d), F32)],
+        scratch_shapes=[pltpu.VMEM((t, d), F32), pltpu.VMEM((t, chunk), BF)],
         compiler_params=pltpu.CompilerParams(vmem_limit_bytes=VMEM),
         cost_estimate=pl.CostEstimate(flops=6 * t * d * ff, bytes_accessed=8 * t * ff, transcendentals=0),
         name="forward",
@@ -475,6 +478,27 @@
     return out[0], out[1:10], out[10:]
 
 
+def adamw_slices(gs, w, m, v, new_w, new_m, new_v, sum_ref):
+    for i in range(3):
+        for j in range(0, gs[0].shape[1], ADAM_ROWS):
+            at = slice(j, j + ADAM_ROWS)
+            g = gs[0][i, at].astype(F32)
+            if sum_ref is not None:
+                total = (g + gs[1][i, at].astype(F32)).astype(BF)
+                sum_ref[i, at] = total
+                g = total.astype(F32)
+            to = (slice(None), at) if i == 2 else (at, slice(None))
+            if i == 2:
+                g = g.T
+            mi = 0.9 * m[i][to] + 0.1 * g
+            vi = 0.95 * v[i][to] + 0.05 * g * g
+            wi = w[i][to].astype(F32)
+            step = mi * lax.rsqrt(vi + 1e-8) + 0.1 * wi
+            new_w[i][to] = (wi - 0.02 * step).astype(BF)
+            new_m[i][to] = mi
+            new_v[i][to] = vi
+
+
 def adamw_kernel(own, aliased, chunks, off_ref, *refs):
     gs, refs = refs[: (1 + own) * chunks], refs[(1 + own) * chunks :]
     w, m, v = refs[0:3], refs[3:6], refs[6:9]
@@ -482,7 +506,7 @@
     new_w, new_m, new_v = refs[0:3], refs[3:6], refs[6:9]
 
     def work(g_refs):
-        adamw_block(g_refs, w, m, v, new_w, new_m, new_v, refs[9] if own else None)
+        adamw_slices(g_refs, w, m, v, new_w, new_m, new_v, refs[9] if own else None)
 
     per = CHUNK // ADAM_COLS
     for k in range(chunks if own else 1):
@@ -527,9 +551,9 @@
 
 
 ORDER = (
-    "p0", "F", "G", "x4", "x5", "Y0", "s0", "t0", "x6", "x7", "Z0", "k0",
-    "x8", "A4+5", "h4", "x9", "C0", "B4+5", "D0", "A6", "h6", "A7", "h7", "B6",
-    "B7", "A8", "h8", "A9", "h9", "B8", "B9",
+    "p0", "F", "G", "x4", "x5", "Y0", "s0", "t0", "x6", "x7", "A4", "h4",
+    "x8", "Z0", "k0", "x9", "A5", "h5", "q9", "B4", "C0", "B5", "D0", "A6+7",
+    "h6", "A8", "h8", "B6+7", "B8", "r9", "A9", "E9",
 )
 
 
@@ -602,6 +626,11 @@
             elif kind == "x":
                 k = int(name[1:]) - NX
                 pair[k][1] = send(pair[k][0], across)
+            elif kind in "qr":
+                have[name] = send(pair[int(name[1:]) - NX][kind == "r"], beside)
+            elif kind == "E":
+                k = int(name[1:])
+                new, _ = adamw(offset(1 - core, k - NEAR), [have[f"q{k}"], have[f"r{k}"]], weights, m, v, new, 0, 1)
             elif kind == "h":
                 have[name[1:]] = send(have["A" + name[1:]], beside)
             else:

time: 827 us -> 869 us (1.051)
  waiting for transfers between devices: 138 us -> 188 us
  Pallas kernels: 670 us -> 659 us
    ppermute x15 -> x16, waiting for transfers between devices: 138 us -> 188 us  [send(): return lax.ppermute(z, AXES, to)]
  transfers between devices with their start and end apart: 15 -> 16, of which waited for: 5 -> 4; matrix products, arithmetic and copies ran while one was open for 0% -> 0% of each run, Pallas kernels for 69% -> 64%
where the time goes in v3:
time: 869 us; the launch traced here: 864 us
  Pallas kernels  659 us (76%)
  waiting for transfers between devices  188 us (22%)
  starting transfers between devices  11.1 us (1%)
    pallas_call x1, Pallas kernels, both(): pl.pallas_call(functools.partial(both_kernel, near, nx), grid=(4 * per,),...  285 us
    ppermute x16, waiting for transfers between devices, send(): return lax.ppermute(z, AXES, to)  188 us
    pallas_call x12, Pallas kernels, adamw(): pl.pallas_call(functools.partial(adamw_kernel, own, new is not None, chun...  161 us
    pallas_call x2, Pallas kernels, shared(): pl.pallas_call(functools.partial(shared_kernel, own, new is not None), gr...  139 us
    pallas_call x1, Pallas kernels, forward(): pl.pallas_call(functools.partial(forward_kernel, rows), grid=(ff // chunk...  73.4 us
  transfers between devices with their start and end apart: 16, of which 4 were waited for; matrix products, arithmetic and copies ran while one was open for 0% of the time, Pallas kernels for 64%

profile of v3, /device:TPU:0, one launch (start us, length us, event | category | flops | bytes accessed | tf_op | source)
XLA Modules:
  0.0 863.7 jit_solution(14834588548227397717)
XLA Ops:
  0.6 3.3 collective-permute-start.6
  4.0 73.4 %forward.1 = (bf16[2048,768]{1,0:T(8,128)(2,1)}, bf16[2048,768]{1,0:T(8,128)(2,1)}, bf16[2048,768]{1,0:T(8,128)(2,1)}, f32[12,2048,512]{2,1,0:T(8,128)}, f32[12,2048,512]{2,1,0:T(8,128)}) custom-call(bf16[2048,768]{1,0:T(8,128)(2,1)} %bitcast.27, bf16[2,768,6144]{2,1,0:T(8,128)(2,1)} %refs_2_.25, bf16[2,768,6144]{2,1,0:T(8,128)(2,1)} %refs_3_.25, ...), custom_call_target="tpu_custom_call" | custom-call | flops 57982058496 | bytes 100663296 | tf_op jit(solution)/shard_map/forward/pallas_call | solution.py:81
  77.3 285.3 %backward.1 = (bf16[4,3,768,512]{3,2,1,0:T(8,128)(2,1)}, bf16[4,3,768,512]{3,2,1,0:T(8,128)(2,1)}, bf16[3,768,512]{2,1,0:T(8,128)(2,1)}, bf16[3,768,512]{2,1,0:T...) custom-call(bf16[2048,768]{1,0:T(8,128)(2,1)} %get-tuple-element.159, ...), custom_call_target="tpu_custom_call" | custom-call | flops 231928233984 | bytes 100663296 | tf_op jit(solution)/shard_map/backward/pallas_call | solution.py:337
  362.8 0.6 concatenate.7.table_ref
  363.4 0.0 collective-permute-done.6.dy_peer
  363.4 72.6 %shared_other.1 = (bf16[3,768,1024]{2,1,0:T(8,128)(2,1)}, bf16[2,768,6144]{2,1,0:T(8,128)(2,1)}, bf16[2,768,6144]{2,1,0:T(8,128)(2,1)}, bf16[2,6144,768]{2,1,0:T...) custom-call(s32[7,8]{1,0:T(8,128)} %concatenate.7.table_ref, ...), custom_call_target="tpu_custom_call" | custom-call | flops 28991029248 | bytes 103809024 | tf_op jit(solution)/shard_map/shared_other/pallas_call | solution.py:458
  436.0 0.0 collective-permute-start.8
  436.0 0.5 collective-permute-start.7
  436.5 0.0 collective-permute-start.9
  436.5 2.0 collective-permute-start.11
  438.6 0.6 concatenate.6.table_ref
  439.2 51.6 %collective-permute-done.9.refs_1_ = bf16[3,768,512]{2,1,0:T(8,128)(2,1)S(1)} collective-permute-done((bf16[3,768,512]{2,1,0:T(8,128)(2,1)}, bf16[3,768,512]{2,1,0:T(8,128)(2,1)S(1)}, u32[]{:S(2)}, u32[]{:S(2)}) %collective-permute-start.9) | collective-permute-done | bytes 2359328 | tf_op jit(solution)/shard_map/ppermute | solution.py:586
  490.8 0.0 copy-start.1
  490.8 1.4 copy-done.1
  492.2 11.1 %adamw_own.6 = (bf16[2,768,6144]{2,1,0:T(8,128)(2,1)}, bf16[2,768,6144]{2,1,0:T(8,128)(2,1)}, bf16[2,6144,768]{2,1,0:T(8,128)(2,1)}, f32[2,768,6144]{2,1,0:T(8,1...) custom-call(s32[1]{0:T(128)} %bitcast.13.off_ref, ...), custom_call_target="tpu_custom_call", output_to_operand_aliasing={{0}: (12, {}), {1}: (13, {}), {2}: (14, {}), {3}: (15, {}),... | custom-call | flops 283115520 | bytes 25952256 | tf_op jit(solution)/shard_map/adamw_own/pallas_call | solution.py:534
  503.3 0.0 collective-permute-done.7.refs_0_
  503.3 0.0 collective-permute-done.8.refs_1_
  503.3 66.9 %shared_own.1 = (bf16[3,768,1024]{2,1,0:T(8,128)(2,1)}, bf16[2,768,6144]{2,1,0:T(8,128)(2,1)}, bf16[2,768,6144]{2,1,0:T(8,128)(2,1)}, bf16[2,6144,768]{2,1,0:T(8...) custom-call(s32[7,8]{1,0:T(8,128)} %concatenate.6.table_ref, ...), custom_call_target="tpu_custom_call", output_to_operand_aliasing={{1}: (22, {}), {2}: (23, {}), {3}: (24, {}), {4}: (25, {}),... | custom-call | flops 28991029248 | bytes 103809024 | tf_op jit(solution)/shard_map/shared_own/pallas_call | solution.py:458
  570.2 0.0 collective-permute-start.10
  570.2 0.5 collective-permute-start.13
  570.7 0.0 collective-permute-done.11.refs_1_
  570.7 11.4 %adamw_own.7 = (bf16[2,768,6144]{2,1,0:T(8,128)(2,1)}, bf16[2,768,6144]{2,1,0:T(8,128)(2,1)}, bf16[2,6144,768]{2,1,0:T(8,128)(2,1)}, f32[2,768,6144]{2,1,0:T(8,1...) custom-call(s32[1]{0:T(128)} %bitcast.15.off_ref, ...), custom_call_target="tpu_custom_call", output_to_operand_aliasing={{0}: (12, {}), {1}: (13, {}), {2}: (14, {}), {3}: (15, {}),... | custom-call | flops 283115520 | bytes 25952256 | tf_op jit(solution)/shard_map/adamw_own/pallas_call | solution.py:534
  582.1 0.0 collective-permute-start.12
  582.1 0.1 collective-permute-start.4
  582.2 2.0 collective-permute-start.5
  584.2 0.0 collective-permute-done.13.refs_0_
  584.2 9.6 %adamw_other.6 = (bf16[2,768,6144]{2,1,0:T(8,128)(2,1)}, bf16[2,768,6144]{2,1,0:T(8,128)(2,1)}, bf16[2,6144,768]{2,1,0:T(8,128)(2,1)}, f32[2,768,6144]{2,1,0:T(8...) custom-call(s32[1]{0:T(128)} %bitcast.16.off_ref, ...), custom_call_target="tpu_custom_call", output_to_operand_aliasing={{0}: (11, {}), {1}: (12, {}), {2}: (13, {}), {3}: (14, {}),... | custom-call | flops 283115520 | bytes 25952256 | tf_op jit(solution)/shard_map/adamw_other/pallas_call | solution.py:534
  593.8 18.0 %adamw_other.7 = (bf16[2,768,6144]{2,1,0:T(8,128)(2,1)}, bf16[2,768,6144]{2,1,0:T(8,128)(2,1)}, bf16[2,6144,768]{2,1,0:T(8,128)(2,1)}, f32[2,768,6144]{2,1,0:T(8...) custom-call(s32[1]{0:T(128)} %bitcast.5.off_ref, ...), custom_call_target="tpu_custom_call", output_to_operand_aliasing={{0}: (11, {}), {1}: (12, {}), {2}: (13, {}), {3}: (14, {}),... | custom-call | flops 566231040 | bytes 51904512 | tf_op jit(solution)/shard_map/adamw_other/pallas_call | solution.py:534
  611.8 0.0 collective-permute-done.12.refs_0_
  611.8 9.4 %adamw_other.8 = (bf16[2,768,6144]{2,1,0:T(8,128)(2,1)}, bf16[2,768,6144]{2,1,0:T(8,128)(2,1)}, bf16[2,6144,768]{2,1,0:T(8,128)(2,1)}, f32[2,768,6144]{2,1,0:T(8...) custom-call(s32[1]{0:T(128)} %bitcast.14.off_ref, ...), custom_call_target="tpu_custom_call", output_to_operand_aliasing={{0}: (11, {}), {1}: (12, {}), {2}: (13, {}), {3}: (14, {}),... | custom-call | flops 283115520 | bytes 25952256 | tf_op jit(solution)/shard_map/adamw_other/pallas_call | solution.py:534
  621.2 0.0 collective-permute-done.10.refs_0_
  621.2 18.2 %adamw_other.9 = (bf16[2,768,6144]{2,1,0:T(8,128)(2,1)}, bf16[2,768,6144]{2,1,0:T(8,128)(2,1)}, bf16[2,6144,768]{2,1,0:T(8,128)(2,1)}, f32[2,768,6144]{2,1,0:T(8...) custom-call(s32[1]{0:T(128)} %bitcast.4.off_ref, ...), custom_call_target="tpu_custom_call", output_to_operand_aliasing={{0}: (11, {}), {1}: (12, {}), {2}: (13, {}), {3}: (14, {}),... | custom-call | flops 566231040 | bytes 51904512 | tf_op jit(solution)/shard_map/adamw_other/pallas_call | solution.py:534
  639.5 0.0 collective-permute-done.4.refs_1_
  639.5 47.2 %collective-permute-done.5.refs_3_ = bf16[3,768,512]{2,1,0:T(8,128)(2,1)} collective-permute-done((bf16[3,768,512]{2,1,0:T(8,128)(2,1)}, bf16[3,768,512]{2,1,0:T(8,128)(2,1)}, u32[]{:S(2)}, u32[]{:S(2)}) %collective-permute-start.5) | collective-permute-done | bytes 2359328 | tf_op jit(solution)/shard_map/ppermute | solution.py:586
  686.6 0.0 copy-start
  686.6 21.4 %adamw_own.8 = (bf16[2,768,6144]{2,1,0:T(8,128)(2,1)}, bf16[2,768,6144]{2,1,0:T(8,128)(2,1)}, bf16[2,6144,768]{2,1,0:T(8,128)(2,1)}, f32[2,768,6144]{2,1,0:T(8,1...) custom-call(s32[1]{0:T(128)} %bitcast.6.off_ref, ...), custom_call_target="tpu_custom_call", output_to_operand_aliasing={{0}: (14, {}), {1}: (15, {}), {2}: (16, {}), {3}: (17, {}),... | custom-call | flops 566231040 | bytes 51904512 | tf_op jit(solution)/shard_map/adamw_own/pallas_call | solution.py:534
  708.1 0.0 collective-permute-start.15
  708.1 0.0 copy-done
  708.1 0.3 collective-permute-start.3
  708.4 1.7 collective-permute-start.1
  710.2 52.1 %collective-permute-done.3.refs_1_ = bf16[3,768,512]{2,1,0:T(8,128)(2,1)S(1)} collective-permute-done((bf16[3,768,512]{2,1,0:T(8,128)(2,1)S(1)}, bf16[3,768,512]{2,1,0:T(8,128)(2,1)S(1)}, u32[]{:S(2)}, u32[]{:S(2)}) %collective-permute-start.3) | collective-permute-done | bytes 2359328 | tf_op jit(solution)/shard_map/ppermute | solution.py:586
  762.3 0.0 copy-start.2
  762.3 1.4 copy-done.2
  763.7 11.3 %adamw_own.9 = (bf16[2,768,6144]{2,1,0:T(8,128)(2,1)}, bf16[2,768,6144]{2,1,0:T(8,128)(2,1)}, bf16[2,6144,768]{2,1,0:T(8,128)(2,1)}, f32[2,768,6144]{2,1,0:T(8,1...) custom-call(s32[1]{0:T(128)} %bitcast.5.off_ref, ...), custom_call_target="tpu_custom_call", output_to_operand_aliasing={{0}: (12, {}), {1}: (13, {}), {2}: (14, {}), {3}: (15, {}),... | custom-call | flops 283115520 | bytes 25952256 | tf_op jit(solution)/shard_map/adamw_own/pallas_call | solution.py:534
  775.1 0.0 collective-permute-start.14
  775.1 0.5 collective-permute-start
  775.6 36.8 %collective-permute-done.1.refs_1_ = bf16[3,768,512]{2,1,0:T(8,128)(2,1)} collective-permute-done((bf16[3,768,512]{2,1,0:T(8,128)(2,1)}, bf16[3,768,512]{2,1,0:T(8,128)(2,1)}, u32[]{:S(2)}, u32[]{:S(2)}) %collective-permute-start.1) | collective-permute-done | bytes 2359328 | tf_op jit(solution)/shard_map/ppermute | solution.py:586
  812.4 0.0 collective-permute-start.2
  812.4 0.0 collective-permute-done.15.refs_0_
  812.4 18.2 %adamw_other.10 = (bf16[2,768,6144]{2,1,0:T(8,128)(2,1)}, bf16[2,768,6144]{2,1,0:T(8,128)(2,1)}, bf16[2,6144,768]{2,1,0:T(8,128)(2,1)}, f32[2,768,6144]{2,1,0:T(...) custom-call(s32[1]{0:T(128)} %bitcast.17.off_ref, ...), custom_call_target="tpu_custom_call", output_to_operand_aliasing={{0}: (11, {}), {1}: (12, {}), {2}: (13, {}), {3}: (14, {}),... | custom-call | flops 566231040 | bytes 51904512 | tf_op jit(solution)/shard_map/adamw_other/pallas_call | solution.py:534
  830.7 0.0 collective-permute-done.14.refs_0_
  830.7 9.6 %adamw_other.11 = (bf16[2,768,6144]{2,1,0:T(8,128)(2,1)}, bf16[2,768,6144]{2,1,0:T(8,128)(2,1)}, bf16[2,6144,768]{2,1,0:T(8,128)(2,1)}, f32[2,768,6144]{2,1,0:T(...) custom-call(s32[1]{0:T(128)} %bitcast.4.off_ref, ...), custom_call_target="tpu_custom_call", output_to_operand_aliasing={{0}: (11, {}), {1}: (12, {}), {2}: (13, {}), {3}: (14, {}),... | custom-call | flops 283115520 | bytes 25952256 | tf_op jit(solution)/shard_map/adamw_other/pallas_call | solution.py:534
  840.3 11.4 %adamw_own.10 = (bf16[2,768,6144]{2,1,0:T(8,128)(2,1)}, bf16[2,768,6144]{2,1,0:T(8,128)(2,1)}, bf16[2,6144,768]{2,1,0:T(8,128)(2,1)}, f32[2,768,6144]{2,1,0:T(8,...) custom-call(s32[1]{0:T(128)} %bitcast.3.off_ref, ...), custom_call_target="tpu_custom_call", output_to_operand_aliasing={{0}: (12, {}), {1}: (13, {}), {2}: (14, {}), {3}: (15, {}),... | custom-call | flops 283115520 | bytes 25952256 | tf_op jit(solution)/shard_map/adamw_own/pallas_call | solution.py:534
  851.8 0.0 collective-permute-done.refs_0_
  851.8 0.0 collective-permute-done.2.refs_1_
  851.8 11.4 %adamw_own.11 = (bf16[2,768,6144]{2,1,0:T(8,128)(2,1)}, bf16[2,768,6144]{2,1,0:T(8,128)(2,1)}, bf16[2,6144,768]{2,1,0:T(8,128)(2,1)}, f32[2,768,6144]{2,1,0:T(8,...) custom-call(s32[1]{0:T(128)} %bitcast.off_ref, ...), custom_call_target="tpu_custom_call", output_to_operand_aliasing={{0}: (12, {}), {1}: (13, {}), {2}: (14, {}), {3}: (15, {}),... | custom-call | flops 283115520 | bytes 25952256 | tf_op jit(solution)/shard_map/adamw_own/pallas_call | solution.py:534
  (11 shorter events, 0.1 us)
Async XLA Ops:
  0.6 362.7 %collective-permute-start.6 = (bf16[2048,768]{1,0:T(8,128)(2,1)}, bf16[2048,768]{1,0:T(8,128)(2,1)}, u32[]{:S(2)}, u32[]{:S(2)}) collective-permute-start(bf16[2048,768]{1,0:T(8,128)(2,1)} %bitcast.23), channel_id=1, source_target_pairs={{0,2},{1,3},{2,0},{3,1},{4,6},{5,7},{6,4},{7,5}} | collective-permute-start | bytes 9437192 | tf_op jit(solution)/shard_map/ppermute | solution.py:586
  436.0 67.3 %collective-permute-start.8 = (bf16[4,3,768,512]{3,2,1,0:T(8,128)(2,1)}, bf16[4,3,768,512]{3,2,1,0:T(8,128)(2,1)}, u32[]{:S(2)}, u32[]{:S(2)}) collective-permute-start(bf16[4,3,768,512]{3,2,1,0:T(8,128)(2,1)} %get-tuple-element.175), channel_id=1, source_target_pairs={{0,1},{1,0},{2,3},{3,2},{4,5},{5,4},{6,7},{7,6}} | collective-permute-start | bytes 28311560 | tf_op jit(solution)/shard_map/ppermute | solution.py:586
  436.0 67.3 %collective-permute-start.7 = (bf16[3,768,1024]{2,1,0:T(8,128)(2,1)}, bf16[3,768,1024]{2,1,0:T(8,128)(2,1)}, u32[]{:S(2)}, u32[]{:S(2)}) collective-permute-start(bf16[3,768,1024]{2,1,0:T(8,128)(2,1)} %get-tuple-element.174), channel_id=1, source_target_pairs={{0,1},{1,0},{2,3},{3,2},{4,5},{5,4},{6,7},{7,6}} | collective-permute-start | bytes 14155784 | tf_op jit(solution)/shard_map/ppermute | solution.py:586
  436.5 54.3 %collective-permute-start.9 = (bf16[3,768,512]{2,1,0:T(8,128)(2,1)}, bf16[3,768,512]{2,1,0:T(8,128)(2,1)S(1)}, u32[]{:S(2)}, u32[]{:S(2)}) collective-permute-start(bf16[3,768,512]{2,1,0:T(8,128)(2,1)} %get-tuple-element.176.refs_0_), channel_id=1, source_target_pairs={{0,2},{1,3},{2,0},{3,1},{4,6},{5,7},{6,4},{7,5}} | collective-permute-start | bytes 7077896 | tf_op jit(solution)/shard_map/ppermute | solution.py:586
  436.5 134.2 %collective-permute-start.11 = (bf16[3,768,512]{2,1,0:T(8,128)(2,1)}, bf16[3,768,512]{2,1,0:T(8,128)(2,1)}, u32[]{:S(2)}, u32[]{:S(2)}) collective-permute-start(bf16[3,768,512]{2,1,0:T(8,128)(2,1)} %get-tuple-element.196.refs_0_), channel_id=1, source_target_pairs={{0,2},{1,3},{2,0},{3,1},{4,6},{5,7},{6,4},{7,5}} | collective-permute-start | bytes 7077896 | tf_op jit(solution)/shard_map/ppermute | solution.py:586
  490.8 1.4 copy-start.1
  570.2 51.0 %collective-permute-start.10 = (bf16[3,768,1024]{2,1,0:T(8,128)(2,1)}, bf16[3,768,1024]{2,1,0:T(8,128)(2,1)}, u32[]{:S(2)}, u32[]{:S(2)}) collective-permute-start(bf16[3,768,1024]{2,1,0:T(8,128)(2,1)} %get-tuple-element.195.refs_0_), channel_id=1, source_target_pairs={{0,1},{1,0},{2,3},{3,2},{4,5},{5,4},{6,7},{7,6}} | collective-permute-start | bytes 14155784 | tf_op jit(solution)/shard_map/ppermute | solution.py:586
  570.2 14.0 %collective-permute-start.13 = (bf16[3,768,512]{2,1,0:T(8,128)(2,1)}, bf16[3,768,512]{2,1,0:T(8,128)(2,1)}, u32[]{:S(2)}, u32[]{:S(2)}) collective-permute-start(bf16[3,768,512]{2,1,0:T(8,128)(2,1)} %get-tuple-element.207), channel_id=1, source_target_pairs={{0,1},{1,0},{2,3},{3,2},{4,5},{5,4},{6,7},{7,6}} | collective-permute-start | bytes 7077896 | tf_op jit(solution)/shard_map/ppermute | solution.py:586
  582.1 29.7 %collective-permute-start.12 = (bf16[3,768,512]{2,1,0:T(8,128)(2,1)}, bf16[3,768,512]{2,1,0:T(8,128)(2,1)}, u32[]{:S(2)}, u32[]{:S(2)}) collective-permute-start(bf16[3,768,512]{2,1,0:T(8,128)(2,1)} %get-tuple-element.206), channel_id=1, source_target_pairs={{0,1},{1,0},{2,3},{3,2},{4,5},{5,4},{6,7},{7,6}} | collective-permute-start | bytes 7077896 | tf_op jit(solution)/shard_map/ppermute | solution.py:586
  582.1 57.3 %collective-permute-start.4 = (bf16[3,768,512]{2,1,0:T(8,128)(2,1)}, bf16[3,768,512]{2,1,0:T(8,128)(2,1)}, u32[]{:S(2)}, u32[]{:S(2)}) collective-permute-start(bf16[3,768,512]{2,1,0:T(8,128)(2,1)} %get-tuple-element.166.refs_0_), channel_id=1, source_target_pairs={{0,2},{1,3},{2,0},{3,1},{4,6},{5,7},{6,4},{7,5}} | collective-permute-start | bytes 7077896 | tf_op jit(solution)/shard_map/ppermute | solution.py:586
  582.2 104.5 %collective-permute-start.5 = (bf16[3,768,512]{2,1,0:T(8,128)(2,1)}, bf16[3,768,512]{2,1,0:T(8,128)(2,1)}, u32[]{:S(2)}, u32[]{:S(2)}) collective-permute-start(bf16[3,768,512]{2,1,0:T(8,128)(2,1)} %get-tuple-element.167.refs_2_), channel_id=1, source_target_pairs={{0,2},{1,3},{2,0},{3,1},{4,6},{5,7},{6,4},{7,5}} | collective-permute-start | bytes 7077896 | tf_op jit(solution)/shard_map/ppermute | solution.py:586
  686.6 21.5 %copy-start = (bf16[3,768,512]{2,1,0:T(8,128)(2,1)S(1)}, bf16[3,768,512]{2,1,0:T(8,128)(2,1)}, u32[]{:S(2)}) copy-start(bf16[3,768,512]{2,1,0:T(8,128)(2,1)} %get-tuple-element.165.refs_0_) | copy-start | bytes 7077892
  708.1 104.4 %collective-permute-start.15 = (bf16[3,768,1024]{2,1,0:T(8,128)(2,1)}, bf16[3,768,1024]{2,1,0:T(8,128)(2,1)}, u32[]{:S(2)}, u32[]{:S(2)}) collective-permute-start(bf16[3,768,1024]{2,1,0:T(8,128)(2,1)} %get-tuple-element.263), channel_id=1, source_target_pairs={{0,1},{1,0},{2,3},{3,2},{4,5},{5,4},{6,7},{7,6}} | collective-permute-start | bytes 14155784 | tf_op jit(solution)/shard_map/ppermute | solution.py:586
  708.1 54.1 %collective-permute-start.3 = (bf16[3,768,512]{2,1,0:T(8,128)(2,1)S(1)}, bf16[3,768,512]{2,1,0:T(8,128)(2,1)S(1)}, u32[]{:S(2)}, u32[]{:S(2)}) collective-permute-start(bf16[3,768,512]{2,1,0:T(8,128)(2,1)S(1)} %copy-done), channel_id=1, source_target_pairs={{0,2},{1,3},{2,0},{3,1},{4,6},{5,7},{6,4},{7,5}} | collective-permute-start | bytes 7077896 | tf_op jit(solution)/shard_map/ppermute | solution.py:586
  708.4 104.0 %collective-permute-start.1 = (bf16[3,768,512]{2,1,0:T(8,128)(2,1)}, bf16[3,768,512]{2,1,0:T(8,128)(2,1)}, u32[]{:S(2)}, u32[]{:S(2)}) collective-permute-start(bf16[3,768,512]{2,1,0:T(8,128)(2,1)} %get-tuple-element.164.refs_0_), channel_id=1, source_target_pairs={{0,2},{1,3},{2,0},{3,1},{4,6},{5,7},{6,4},{7,5}} | collective-permute-start | bytes 7077896 | tf_op jit(solution)/shard_map/ppermute | solution.py:586
  762.3 1.4 copy-start.2
  775.1 55.6 %collective-permute-start.14 = (bf16[3,768,512]{2,1,0:T(8,128)(2,1)}, bf16[3,768,512]{2,1,0:T(8,128)(2,1)}, u32[]{:S(2)}, u32[]{:S(2)}) collective-permute-start(bf16[3,768,512]{2,1,0:T(8,128)(2,1)} %get-tuple-element.262), channel_id=1, source_target_pairs={{0,1},{1,0},{2,3},{3,2},{4,5},{5,4},{6,7},{7,6}} | collective-permute-start | bytes 7077896 | tf_op jit(solution)/shard_map/ppermute | solution.py:586
  775.1 76.7 %collective-permute-start = (bf16[3,768,512]{2,1,0:T(8,128)(2,1)}, bf16[3,768,512]{2,1,0:T(8,128)(2,1)}, u32[]{:S(2)}, u32[]{:S(2)}) collective-permute-start(bf16[3,768,512]{2,1,0:T(8,128)(2,1)} %get-tuple-element.164.refs_0_), channel_id=1, source_target_pairs={{0,1},{1,0},{2,3},{3,2},{4,5},{5,4},{6,7},{7,6}} | collective-permute-start | bytes 7077896 | tf_op jit(solution)/shard_map/ppermute | solution.py:586
  812.4 39.4 %collective-permute-start.2 = (bf16[3,768,512]{2,1,0:T(8,128)(2,1)}, bf16[3,768,512]{2,1,0:T(8,128)(2,1)}, u32[]{:S(2)}, u32[]{:S(2)}) collective-permute-start(bf16[3,768,512]{2,1,0:T(8,128)(2,1)} %collective-permute-done.1.refs_1_), channel_id=1, source_target_pairs={{0,1},{1,0},{2,3},{3,2},{4,5},{5,4},{6,7},{7,6}} | collective-permute-start | bytes 7077896 | tf_op jit(solution)/shard_map/ppermute | solution.py:586

commit v4 on v3

--- a/solution.py
+++ b/solution.py
@@ -552,8 +552,9 @@
 
 ORDER = (
     "p0", "F", "G", "x4", "x5", "Y0", "s0", "t0", "x6", "x7", "A4", "h4",
-    "x8", "Z0", "k0", "x9", "A5", "h5", "q9", "B4", "C0", "B5", "D0", "A6+7",
-    "h6", "A8", "h8", "B6+7", "B8", "r9", "A9", "E9",
+    "x8", "Z0", "k0", "y0", "y1", "A5", "h5", "v0", "v1", "B4", "C0", "B5",
+    "D0", "A6+7", "h6", "A8", "h8", "B6+7", "B8", "u0", "M0", "N0", "u1", "M1",
+    "N1",
 )
 
 
@@ -626,11 +627,16 @@
             elif kind == "x":
                 k = int(name[1:]) - NX
                 pair[k][1] = send(pair[k][0], across)
-            elif kind in "qr":
-                have[name] = send(pair[int(name[1:]) - NX][kind == "r"], beside)
-            elif kind == "E":
-                k = int(name[1:])
-                new, _ = adamw(offset(1 - core, k - NEAR), [have[f"q{k}"], have[f"r{k}"]], weights, m, v, new, 0, 1)
+            elif kind in "yv":
+                i = int(name[1:]) * ADAM_COLS
+                have[name] = send(pair[-1][0][:, :, i : i + ADAM_COLS], across if kind == "y" else beside)
+            elif kind == "u":
+                have[name] = send(have["y" + name[1:]], beside)
+            elif kind in "MN":
+                i, side = int(name[1:]), core if kind == "M" else 1 - core
+                mine = pair[-1][0][:, :, i * ADAM_COLS : (i + 1) * ADAM_COLS]
+                gs = [mine, have[f"y{i}"]] if kind == "M" else [have[f"v{i}"], have[f"u{i}"]]
+                new, _ = adamw(offset(side, per - 1) + i, gs, weights, m, v, new, 0, 1)
             elif kind == "h":
                 have[name[1:]] = send(have["A" + name[1:]], beside)
             else:

time: 869 us -> 893 us (1.028)
  waiting for transfers between devices: 188 us -> 204 us
    ppermute x16 -> x19, waiting for transfers between devices: 188 us -> 204 us  [send(): return lax.ppermute(z, AXES, to)]
    pallas_call x12 -> x14, Pallas kernels: 161 us -> 167 us  [adamw(): pl.pallas_call(functools.partial(adamw_kernel, own, new is not None, chun...]
  transfers between devices with their start and end apart: 16 -> 19, of which waited for: 4 -> 5; matrix products, arithmetic and copies ran while one was open for 0% -> 0% of each run, Pallas kernels for 64% -> 64%
where the time goes in v4:
time: 893 us; the launch traced here: 888 us
  Pallas kernels  665 us (74%)
  waiting for transfers between devices  204 us (23%)
  starting transfers between devices  11.4 us (1%)
    pallas_call x1, Pallas kernels, both(): pl.pallas_call(functools.partial(both_kernel, near, nx), grid=(4 * per,),...  285 us
    ppermute x19, waiting for transfers between devices, send(): return lax.ppermute(z, AXES, to)  204 us
    pallas_call x14, Pallas kernels, adamw(): pl.pallas_call(functools.partial(adamw_kernel, own, new is not None, chun...  167 us
    pallas_call x2, Pallas kernels, shared(): pl.pallas_call(functools.partial(shared_kernel, own, new is not None), gr...  139 us
    pallas_call x1, Pallas kernels, forward(): pl.pallas_call(functools.partial(forward_kernel, rows), grid=(ff // chunk...  73.4 us
  transfers between devices with their start and end apart: 19, of which 5 were waited for; matrix products, arithmetic and copies ran while one was open for 0% of the time, Pallas kernels for 64%

profile of v4, /device:TPU:0, one launch (start us, length us, event | category | flops | bytes accessed | tf_op | source)
XLA Modules:
  0.0 887.8 jit_solution(17963238390511576349)
XLA Ops:
  0.6 3.3 collective-permute-start.9
  4.0 73.4 %forward.1 = (bf16[2048,768]{1,0:T(8,128)(2,1)}, bf16[2048,768]{1,0:T(8,128)(2,1)}, bf16[2048,768]{1,0:T(8,128)(2,1)}, f32[12,2048,512]{2,1,0:T(8,128)}, f32[12,2048,512]{2,1,0:T(8,128)}) custom-call(bf16[2048,768]{1,0:T(8,128)(2,1)} %bitcast.27, bf16[2,768,6144]{2,1,0:T(8,128)(2,1)} %refs_2_.29, bf16[2,768,6144]{2,1,0:T(8,128)(2,1)} %refs_3_.29, ...), custom_call_target="tpu_custom_call" | custom-call | flops 57982058496 | bytes 100663296 | tf_op jit(solution)/shard_map/forward/pallas_call | solution.py:81
  77.4 285.3 %backward.1 = (bf16[4,3,768,512]{3,2,1,0:T(8,128)(2,1)}, bf16[4,3,768,512]{3,2,1,0:T(8,128)(2,1)}, bf16[3,768,512]{2,1,0:T(8,128)(2,1)}, bf16[3,768,512]{2,1,0:T...) custom-call(bf16[2048,768]{1,0:T(8,128)(2,1)} %get-tuple-element.177, ...), custom_call_target="tpu_custom_call" | custom-call | flops 231928233984 | bytes 100663296 | tf_op jit(solution)/shard_map/backward/pallas_call | solution.py:337
  362.8 0.6 concatenate.7.table_ref
  363.4 0.0 collective-permute-done.9.dy_peer
  363.4 72.6 %shared_other.1 = (bf16[3,768,1024]{2,1,0:T(8,128)(2,1)}, bf16[2,768,6144]{2,1,0:T(8,128)(2,1)}, bf16[2,768,6144]{2,1,0:T(8,128)(2,1)}, bf16[2,6144,768]{2,1,0:T...) custom-call(s32[7,8]{1,0:T(8,128)} %concatenate.7.table_ref, ...), custom_call_target="tpu_custom_call" | custom-call | flops 28991029248 | bytes 103809024 | tf_op jit(solution)/shard_map/shared_other/pallas_call | solution.py:458
  436.0 0.0 collective-permute-start.11
  436.0 0.5 collective-permute-start.10
  436.5 0.0 collective-permute-start.12
  436.6 2.0 collective-permute-start.14
  438.6 0.6 concatenate.6.table_ref
  439.2 51.6 %collective-permute-done.12.refs_1_ = bf16[3,768,512]{2,1,0:T(8,128)(2,1)S(1)} collective-permute-done((bf16[3,768,512]{2,1,0:T(8,128)(2,1)}, bf16[3,768,512]{2,1,0:T(8,128)(2,1)S(1)}, u32[]{:S(2)}, u32[]{:S(2)}) %collective-permute-start.12) | collective-permute-done | bytes 2359328 | tf_op jit(solution)/shard_map/ppermute | solution.py:587
  490.9 0.0 copy-start.1
  490.9 1.4 copy-done.1
  492.2 11.2 %adamw_own.8 = (bf16[2,768,6144]{2,1,0:T(8,128)(2,1)}, bf16[2,768,6144]{2,1,0:T(8,128)(2,1)}, bf16[2,6144,768]{2,1,0:T(8,128)(2,1)}, f32[2,768,6144]{2,1,0:T(8,1...) custom-call(s32[1]{0:T(128)} %bitcast.13.off_ref, ...), custom_call_target="tpu_custom_call", output_to_operand_aliasing={{0}: (12, {}), {1}: (13, {}), {2}: (14, {}), {3}: (15, {}),... | custom-call | flops 283115520 | bytes 25952256 | tf_op jit(solution)/shard_map/adamw_own/pallas_call | solution.py:534
  503.4 0.0 collective-permute-done.10.refs_0_
  503.4 0.0 collective-permute-done.11.refs_1_
  503.4 66.9 %shared_own.1 = (bf16[3,768,1024]{2,1,0:T(8,128)(2,1)}, bf16[2,768,6144]{2,1,0:T(8,128)(2,1)}, bf16[2,768,6144]{2,1,0:T(8,128)(2,1)}, bf16[2,6144,768]{2,1,0:T(8...) custom-call(s32[7,8]{1,0:T(8,128)} %concatenate.6.table_ref, ...), custom_call_target="tpu_custom_call", output_to_operand_aliasing={{1}: (22, {}), {2}: (23, {}), {3}: (24, {}), {4}: (25, {}),... | custom-call | flops 28991029248 | bytes 103809024 | tf_op jit(solution)/shard_map/shared_own/pallas_call | solution.py:458
  570.3 0.0 collective-permute-start.13
  570.3 0.5 collective-permute-start.16
  570.8 0.0 collective-permute-done.14.refs_1_
  570.8 11.4 %adamw_own.9 = (bf16[2,768,6144]{2,1,0:T(8,128)(2,1)}, bf16[2,768,6144]{2,1,0:T(8,128)(2,1)}, bf16[2,6144,768]{2,1,0:T(8,128)(2,1)}, f32[2,768,6144]{2,1,0:T(8,1...) custom-call(s32[1]{0:T(128)} %bitcast.15.off_ref, ...), custom_call_target="tpu_custom_call", output_to_operand_aliasing={{0}: (12, {}), {1}: (13, {}), {2}: (14, {}), {3}: (15, {}),... | custom-call | flops 283115520 | bytes 25952256 | tf_op jit(solution)/shard_map/adamw_own/pallas_call | solution.py:534
  582.2 0.1 collective-permute-start.15
  582.3 0.0 collective-permute-start.7
  582.3 2.0 collective-permute-start.8
  584.3 0.0 collective-permute-done.16.refs_0_
  584.3 9.6 %adamw_other.6 = (bf16[2,768,6144]{2,1,0:T(8,128)(2,1)}, bf16[2,768,6144]{2,1,0:T(8,128)(2,1)}, bf16[2,6144,768]{2,1,0:T(8,128)(2,1)}, f32[2,768,6144]{2,1,0:T(8...) custom-call(s32[1]{0:T(128)} %bitcast.16.off_ref, ...), custom_call_target="tpu_custom_call", output_to_operand_aliasing={{0}: (11, {}), {1}: (12, {}), {2}: (13, {}), {3}: (14, {}),... | custom-call | flops 283115520 | bytes 25952256 | tf_op jit(solution)/shard_map/adamw_other/pallas_call | solution.py:534
  594.0 18.0 %adamw_other.7 = (bf16[2,768,6144]{2,1,0:T(8,128)(2,1)}, bf16[2,768,6144]{2,1,0:T(8,128)(2,1)}, bf16[2,6144,768]{2,1,0:T(8,128)(2,1)}, f32[2,768,6144]{2,1,0:T(8...) custom-call(s32[1]{0:T(128)} %bitcast.5.off_ref, ...), custom_call_target="tpu_custom_call", output_to_operand_aliasing={{0}: (11, {}), {1}: (12, {}), {2}: (13, {}), {3}: (14, {}),... | custom-call | flops 566231040 | bytes 51904512 | tf_op jit(solution)/shard_map/adamw_other/pallas_call | solution.py:534
  612.0 0.0 collective-permute-done.15.refs_0_
  612.0 9.4 %adamw_other.8 = (bf16[2,768,6144]{2,1,0:T(8,128)(2,1)}, bf16[2,768,6144]{2,1,0:T(8,128)(2,1)}, bf16[2,6144,768]{2,1,0:T(8,128)(2,1)}, f32[2,768,6144]{2,1,0:T(8...) custom-call(s32[1]{0:T(128)} %bitcast.14.off_ref, ...), custom_call_target="tpu_custom_call", output_to_operand_aliasing={{0}: (11, {}), {1}: (12, {}), {2}: (13, {}), {3}: (14, {}),... | custom-call | flops 283115520 | bytes 25952256 | tf_op jit(solution)/shard_map/adamw_other/pallas_call | solution.py:534
  621.4 0.0 collective-permute-done.13.refs_0_
  621.4 18.2 %adamw_other.9 = (bf16[2,768,6144]{2,1,0:T(8,128)(2,1)}, bf16[2,768,6144]{2,1,0:T(8,128)(2,1)}, bf16[2,6144,768]{2,1,0:T(8,128)(2,1)}, f32[2,768,6144]{2,1,0:T(8...) custom-call(s32[1]{0:T(128)} %bitcast.4.off_ref, ...), custom_call_target="tpu_custom_call", output_to_operand_aliasing={{0}: (11, {}), {1}: (12, {}), {2}: (13, {}), {3}: (14, {}),... | custom-call | flops 566231040 | bytes 51904512 | tf_op jit(solution)/shard_map/adamw_other/pallas_call | solution.py:534
  639.7 0.0 collective-permute-done.7.refs_1_
  639.7 47.1 %collective-permute-done.8.refs_3_ = bf16[3,768,512]{2,1,0:T(8,128)(2,1)} collective-permute-done((bf16[3,768,512]{2,1,0:T(8,128)(2,1)}, bf16[3,768,512]{2,1,0:T(8,128)(2,1)}, u32[]{:S(2)}, u32[]{:S(2)}) %collective-permute-start.8) | collective-permute-done | bytes 2359328 | tf_op jit(solution)/shard_map/ppermute | solution.py:587
  686.8 21.4 %adamw_own.10 = (bf16[2,768,6144]{2,1,0:T(8,128)(2,1)}, bf16[2,768,6144]{2,1,0:T(8,128)(2,1)}, bf16[2,6144,768]{2,1,0:T(8,128)(2,1)}, f32[2,768,6144]{2,1,0:T(8,...) custom-call(s32[1]{0:T(128)} %bitcast.6.off_ref, ...), custom_call_target="tpu_custom_call", output_to_operand_aliasing={{0}: (14, {}), {1}: (15, {}), {2}: (16, {}), {3}: (17, {}),... | custom-call | flops 566231040 | bytes 51904512 | tf_op jit(solution)/shard_map/adamw_own/pallas_call | solution.py:534
  708.2 0.0 collective-permute-start.18
  708.3 0.0 copy-done
  708.3 0.3 collective-permute-start.6
  708.6 53.3 %collective-permute-done.6.refs_1_ = bf16[3,768,512]{2,1,0:T(8,128)(2,1)S(1)} collective-permute-done((bf16[3,768,512]{2,1,0:T(8,128)(2,1)S(1)}, bf16[3,768,512]{2,1,0:T(8,128)(2,1)S(1)}, u32[]{:S(2)}, u32[]{:S(2)}) %collective-permute-start.6) | collective-permute-done | bytes 2359328 | tf_op jit(solution)/shard_map/ppermute | solution.py:587
  761.9 1.4 copy-done.2
  763.3 11.5 %adamw_own.11 = (bf16[2,768,6144]{2,1,0:T(8,128)(2,1)}, bf16[2,768,6144]{2,1,0:T(8,128)(2,1)}, bf16[2,6144,768]{2,1,0:T(8,128)(2,1)}, f32[2,768,6144]{2,1,0:T(8,...) custom-call(s32[1]{0:T(128)} %bitcast.5.off_ref, ...), custom_call_target="tpu_custom_call", output_to_operand_aliasing={{0}: (12, {}), {1}: (13, {}), {2}: (14, {}), {3}: (15, {}),... | custom-call | flops 283115520 | bytes 25952256 | tf_op jit(solution)/shard_map/adamw_own/pallas_call | solution.py:534
  774.8 0.0 collective-permute-start.17
  774.9 0.0 copy-done.3
  774.9 1.6 fusion
  776.4 0.3 collective-permute-start.4
  776.7 1.7 collective-permute-start.1
  778.5 0.0 collective-permute-start.3
  778.5 27.1 %collective-permute-done.4.refs_1_ = bf16[3,768,256]{2,1,0:T(8,128)(2,1)} collective-permute-done((bf16[3,768,256]{2,1,0:T(8,128)(2,1)}, bf16[3,768,256]{2,1,0:T(8,128)(2,1)}, u32[]{:S(2)}, u32[]{:S(2)}) %collective-permute-start.4) | collective-permute-done | bytes 1179680 | tf_op jit(solution)/shard_map/ppermute | solution.py:587
  805.6 0.0 collective-permute-start.5
  805.6 24.8 %collective-permute-done.1.refs_1_ = bf16[3,768,256]{2,1,0:T(8,128)(2,1)} collective-permute-done((bf16[3,768,256]{2,1,0:T(8,128)(2,1)}, bf16[3,768,256]{2,1,0:T(8,128)(2,1)}, u32[]{:S(2)}, u32[]{:S(2)}) %collective-permute-start.1) | collective-permute-done | bytes 1179680 | tf_op jit(solution)/shard_map/ppermute | solution.py:587
  830.4 0.0 collective-permute-start
  830.4 0.0 collective-permute-done.18.refs_0_
  830.4 0.5 collective-permute-start.2
  830.9 18.2 %adamw_other.10 = (bf16[2,768,6144]{2,1,0:T(8,128)(2,1)}, bf16[2,768,6144]{2,1,0:T(8,128)(2,1)}, bf16[2,6144,768]{2,1,0:T(8,128)(2,1)}, f32[2,768,6144]{2,1,0:T(...) custom-call(s32[1]{0:T(128)} %bitcast.17.off_ref, ...), custom_call_target="tpu_custom_call", output_to_operand_aliasing={{0}: (11, {}), {1}: (12, {}), {2}: (13, {}), {3}: (14, {}),... | custom-call | flops 566231040 | bytes 51904512 | tf_op jit(solution)/shard_map/adamw_other/pallas_call | solution.py:534
  849.1 0.0 collective-permute-done.17.refs_0_
  849.2 9.6 %adamw_other.11 = (bf16[2,768,6144]{2,1,0:T(8,128)(2,1)}, bf16[2,768,6144]{2,1,0:T(8,128)(2,1)}, bf16[2,6144,768]{2,1,0:T(8,128)(2,1)}, f32[2,768,6144]{2,1,0:T(...) custom-call(s32[1]{0:T(128)} %bitcast.4.off_ref, ...), custom_call_target="tpu_custom_call", output_to_operand_aliasing={{0}: (11, {}), {1}: (12, {}), {2}: (13, {}), {3}: (14, {}),... | custom-call | flops 283115520 | bytes 25952256 | tf_op jit(solution)/shard_map/adamw_other/pallas_call | solution.py:534
  858.8 7.1 adamw_own.12
  865.9 0.0 collective-permute-done.3.refs_0_
  865.9 0.0 collective-permute-done.5.refs_1_
  865.9 7.1 adamw_own.13
  873.0 7.1 adamw_own.14
  880.2 0.0 collective-permute-done.refs_0_
  880.2 0.0 collective-permute-done.2.refs_1_
  880.2 7.1 adamw_own.15
  (14 shorter events, 0.1 us)
Async XLA Ops:
  0.6 362.8 %collective-permute-start.9 = (bf16[2048,768]{1,0:T(8,128)(2,1)}, bf16[2048,768]{1,0:T(8,128)(2,1)}, u32[]{:S(2)}, u32[]{:S(2)}) collective-permute-start(bf16[2048,768]{1,0:T(8,128)(2,1)} %bitcast.23), channel_id=1, source_target_pairs={{0,2},{1,3},{2,0},{3,1},{4,6},{5,7},{6,4},{7,5}} | collective-permute-start | bytes 9437192 | tf_op jit(solution)/shard_map/ppermute | solution.py:587
  436.0 67.4 %collective-permute-start.11 = (bf16[4,3,768,512]{3,2,1,0:T(8,128)(2,1)}, bf16[4,3,768,512]{3,2,1,0:T(8,128)(2,1)}, u32[]{:S(2)}, u32[]{:S(2)}) collective-permute-start(bf16[4,3,768,512]{3,2,1,0:T(8,128)(2,1)} %get-tuple-element.193), channel_id=1, source_target_pairs={{0,1},{1,0},{2,3},{3,2},{4,5},{5,4},{6,7},{7,6}} | collective-permute-start | bytes 28311560 | tf_op jit(solution)/shard_map/ppermute | solution.py:587
  436.0 67.4 %collective-permute-start.10 = (bf16[3,768,1024]{2,1,0:T(8,128)(2,1)}, bf16[3,768,1024]{2,1,0:T(8,128)(2,1)}, u32[]{:S(2)}, u32[]{:S(2)}) collective-permute-start(bf16[3,768,1024]{2,1,0:T(8,128)(2,1)} %get-tuple-element.192), channel_id=1, source_target_pairs={{0,1},{1,0},{2,3},{3,2},{4,5},{5,4},{6,7},{7,6}} | collective-permute-start | bytes 14155784 | tf_op jit(solution)/shard_map/ppermute | solution.py:587
  436.5 54.3 %collective-permute-start.12 = (bf16[3,768,512]{2,1,0:T(8,128)(2,1)}, bf16[3,768,512]{2,1,0:T(8,128)(2,1)S(1)}, u32[]{:S(2)}, u32[]{:S(2)}) collective-permute-start(bf16[3,768,512]{2,1,0:T(8,128)(2,1)} %get-tuple-element.194.refs_0_), channel_id=1, source_target_pairs={{0,2},{1,3},{2,0},{3,1},{4,6},{5,7},{6,4},{7,5}} | collective-permute-start | bytes 7077896 | tf_op jit(solution)/shard_map/ppermute | solution.py:587
  436.6 134.3 %collective-permute-start.14 = (bf16[3,768,512]{2,1,0:T(8,128)(2,1)}, bf16[3,768,512]{2,1,0:T(8,128)(2,1)}, u32[]{:S(2)}, u32[]{:S(2)}) collective-permute-start(bf16[3,768,512]{2,1,0:T(8,128)(2,1)} %get-tuple-element.214.refs_0_), channel_id=1, source_target_pairs={{0,2},{1,3},{2,0},{3,1},{4,6},{5,7},{6,4},{7,5}} | collective-permute-start | bytes 7077896 | tf_op jit(solution)/shard_map/ppermute | solution.py:587
  490.9 1.4 copy-start.1
  570.3 51.1 %collective-permute-start.13 = (bf16[3,768,1024]{2,1,0:T(8,128)(2,1)}, bf16[3,768,1024]{2,1,0:T(8,128)(2,1)}, u32[]{:S(2)}, u32[]{:S(2)}) collective-permute-start(bf16[3,768,1024]{2,1,0:T(8,128)(2,1)} %get-tuple-element.213.refs_0_), channel_id=1, source_target_pairs={{0,1},{1,0},{2,3},{3,2},{4,5},{5,4},{6,7},{7,6}} | collective-permute-start | bytes 14155784 | tf_op jit(solution)/shard_map/ppermute | solution.py:587
  570.3 14.0 %collective-permute-start.16 = (bf16[3,768,512]{2,1,0:T(8,128)(2,1)}, bf16[3,768,512]{2,1,0:T(8,128)(2,1)}, u32[]{:S(2)}, u32[]{:S(2)}) collective-permute-start(bf16[3,768,512]{2,1,0:T(8,128)(2,1)} %get-tuple-element.225), channel_id=1, source_target_pairs={{0,1},{1,0},{2,3},{3,2},{4,5},{5,4},{6,7},{7,6}} | collective-permute-start | bytes 7077896 | tf_op jit(solution)/shard_map/ppermute | solution.py:587
  582.2 29.7 %collective-permute-start.15 = (bf16[3,768,512]{2,1,0:T(8,128)(2,1)}, bf16[3,768,512]{2,1,0:T(8,128)(2,1)}, u32[]{:S(2)}, u32[]{:S(2)}) collective-permute-start(bf16[3,768,512]{2,1,0:T(8,128)(2,1)} %get-tuple-element.224), channel_id=1, source_target_pairs={{0,1},{1,0},{2,3},{3,2},{4,5},{5,4},{6,7},{7,6}} | collective-permute-start | bytes 7077896 | tf_op jit(solution)/shard_map/ppermute | solution.py:587
  582.3 57.4 %collective-permute-start.7 = (bf16[3,768,512]{2,1,0:T(8,128)(2,1)}, bf16[3,768,512]{2,1,0:T(8,128)(2,1)}, u32[]{:S(2)}, u32[]{:S(2)}) collective-permute-start(bf16[3,768,512]{2,1,0:T(8,128)(2,1)} %get-tuple-element.184.refs_0_), channel_id=1, source_target_pairs={{0,2},{1,3},{2,0},{3,1},{4,6},{5,7},{6,4},{7,5}} | collective-permute-start | bytes 7077896 | tf_op jit(solution)/shard_map/ppermute | solution.py:587
  582.3 104.5 %collective-permute-start.8 = (bf16[3,768,512]{2,1,0:T(8,128)(2,1)}, bf16[3,768,512]{2,1,0:T(8,128)(2,1)}, u32[]{:S(2)}, u32[]{:S(2)}) collective-permute-start(bf16[3,768,512]{2,1,0:T(8,128)(2,1)} %get-tuple-element.185.refs_2_), channel_id=1, source_target_pairs={{0,2},{1,3},{2,0},{3,1},{4,6},{5,7},{6,4},{7,5}} | collective-permute-start | bytes 7077896 | tf_op jit(solution)/shard_map/ppermute | solution.py:587
  686.8 21.5 %copy-start = (bf16[3,768,512]{2,1,0:T(8,128)(2,1)S(1)}, bf16[3,768,512]{2,1,0:T(8,128)(2,1)}, u32[]{:S(2)}) copy-start(bf16[3,768,512]{2,1,0:T(8,128)(2,1)} %get-tuple-element.183.refs_0_) | copy-start | bytes 7077892
  708.2 122.2 %collective-permute-start.18 = (bf16[3,768,1024]{2,1,0:T(8,128)(2,1)}, bf16[3,768,1024]{2,1,0:T(8,128)(2,1)}, u32[]{:S(2)}, u32[]{:S(2)}) collective-permute-start(bf16[3,768,1024]{2,1,0:T(8,128)(2,1)} %get-tuple-element.281), channel_id=1, source_target_pairs={{0,1},{1,0},{2,3},{3,2},{4,5},{5,4},{6,7},{7,6}} | collective-permute-start | bytes 14155784 | tf_op jit(solution)/shard_map/ppermute | solution.py:587
  708.3 53.6 %collective-permute-start.6 = (bf16[3,768,512]{2,1,0:T(8,128)(2,1)S(1)}, bf16[3,768,512]{2,1,0:T(8,128)(2,1)S(1)}, u32[]{:S(2)}, u32[]{:S(2)}) collective-permute-start(bf16[3,768,512]{2,1,0:T(8,128)(2,1)S(1)} %copy-done), channel_id=1, source_target_pairs={{0,2},{1,3},{2,0},{3,1},{4,6},{5,7},{6,4},{7,5}} | collective-permute-start | bytes 7077896 | tf_op jit(solution)/shard_map/ppermute | solution.py:587
  761.9 1.4 copy-start.2
  763.3 11.5 %copy-start.3 = (bf16[3,768,512]{2,1,0:T(8,128)(2,1)S(1)}, bf16[3,768,512]{2,1,0:T(8,128)(2,1)}, u32[]{:S(2)}) copy-start(bf16[3,768,512]{2,1,0:T(8,128)(2,1)} %get-tuple-element.182) | copy-start | bytes 7077892
  774.8 74.3 %collective-permute-start.17 = (bf16[3,768,512]{2,1,0:T(8,128)(2,1)}, bf16[3,768,512]{2,1,0:T(8,128)(2,1)}, u32[]{:S(2)}, u32[]{:S(2)}) collective-permute-start(bf16[3,768,512]{2,1,0:T(8,128)(2,1)} %get-tuple-element.280), channel_id=1, source_target_pairs={{0,1},{1,0},{2,3},{3,2},{4,5},{5,4},{6,7},{7,6}} | collective-permute-start | bytes 7077896 | tf_op jit(solution)/shard_map/ppermute | solution.py:587
  776.4 29.2 %collective-permute-start.4 = (bf16[3,768,256]{2,1,0:T(8,128)(2,1)}, bf16[3,768,256]{2,1,0:T(8,128)(2,1)}, u32[]{:S(2)}, u32[]{:S(2)}) collective-permute-start(bf16[3,768,256]{2,1,0:T(8,128)(2,1)} %get-tuple-element.345.refs_0_), channel_id=1, source_target_pairs={{0,2},{1,3},{2,0},{3,1},{4,6},{5,7},{6,4},{7,5}} | collective-permute-start | bytes 3538952 | tf_op jit(solution)/shard_map/ppermute | solution.py:587
  776.7 53.7 %collective-permute-start.1 = (bf16[3,768,256]{2,1,0:T(8,128)(2,1)}, bf16[3,768,256]{2,1,0:T(8,128)(2,1)}, u32[]{:S(2)}, u32[]{:S(2)}) collective-permute-start(bf16[3,768,256]{2,1,0:T(8,128)(2,1)} %get-tuple-element.346.refs_0_), channel_id=1, source_target_pairs={{0,2},{1,3},{2,0},{3,1},{4,6},{5,7},{6,4},{7,5}} | collective-permute-start | bytes 3538952 | tf_op jit(solution)/shard_map/ppermute | solution.py:587
  778.5 87.5 %collective-permute-start.3 = (bf16[3,768,256]{2,1,0:T(8,128)(2,1)}, bf16[3,768,256]{2,1,0:T(8,128)(2,1)}, u32[]{:S(2)}, u32[]{:S(2)}) collective-permute-start(bf16[3,768,256]{2,1,0:T(8,128)(2,1)} %get-tuple-element.345.refs_0_), channel_id=1, source_target_pairs={{0,1},{1,0},{2,3},{3,2},{4,5},{5,4},{6,7},{7,6}} | collective-permute-start | bytes 3538952 | tf_op jit(solution)/shard_map/ppermute | solution.py:587
  805.6 60.3 %collective-permute-start.5 = (bf16[3,768,256]{2,1,0:T(8,128)(2,1)}, bf16[3,768,256]{2,1,0:T(8,128)(2,1)}, u32[]{:S(2)}, u32[]{:S(2)}) collective-permute-start(bf16[3,768,256]{2,1,0:T(8,128)(2,1)} %collective-permute-done.4.refs_1_), channel_id=1, source_target_pairs={{0,1},{1,0},{2,3},{3,2},{4,5},{5,4},{6,7},{7,6}} | collective-permute-start | bytes 3538952 | tf_op jit(solution)/shard_map/ppermute | solution.py:587
  830.4 49.8 %collective-permute-start = (bf16[3,768,256]{2,1,0:T(8,128)(2,1)}, bf16[3,768,256]{2,1,0:T(8,128)(2,1)}, u32[]{:S(2)}, u32[]{:S(2)}) collective-permute-start(bf16[3,768,256]{2,1,0:T(8,128)(2,1)} %get-tuple-element.346.refs_0_), channel_id=1, source_target_pairs={{0,1},{1,0},{2,3},{3,2},{4,5},{5,4},{6,7},{7,6}} | collective-permute-start | bytes 3538952 | tf_op jit(solution)/shard_map/ppermute | solution.py:587
  830.4 49.8 %collective-permute-start.2 = (bf16[3,768,256]{2,1,0:T(8,128)(2,1)}, bf16[3,768,256]{2,1,0:T(8,128)(2,1)}, u32[]{:S(2)}, u32[]{:S(2)}) collective-permute-start(bf16[3,768,256]{2,1,0:T(8,128)(2,1)} %collective-permute-done.1.refs_1_), channel_id=1, source_target_pairs={{0,1},{1,0},{2,3},{3,2},{4,5},{5,4},{6,7},{7,6}} | collective-permute-start | bytes 3538952 | tf_op jit(solution)/shard_map/ppermute | solution.py:587
